TPU v7x, 32 devices: a whole 2x2x4 slice. The times are simulated.
32 devices in a mesh: dp: 4 (over y, x), expert: 8 (over z, core).
Axes of the slice: x: 2, y: 2, z: 4, core: 2. Of those that a mesh axis runs over, the one named last changes fastest.
Arguments:
- tokens: bfloat16 [4096, 2048], P(('dp', 'expert')), may hold values from -6 to 6
- expert_ids: int32 [4096, 2], P(('dp', 'expert')), may hold values from 0 to 7, all different within a row; in each aligned block of 128 rows (0 to 127, 128 to 255, ...) at most 48 rows name the same one
- route_weights: float32 [4096, 2], P(('dp', 'expert')), may hold values from 0.1 to 1
- w_gate: bfloat16 [8, 2048, 384], P('expert', 'dp'), may hold values from -0.125 to 0.125
- w_up: bfloat16 [8, 2048, 384], P('expert', 'dp'), may hold values from -0.125 to 0.125
- w_down: bfloat16 [8, 2048, 384], P('expert', 'dp'), may hold values from -0.3125 to 0.3125
- grad_out: bfloat16 [4096, 2048], P(('dp', 'expert')), may hold values from -6 to 6
Outputs:
- layer_out: bfloat16 [4096, 2048], P(('dp', 'expert'))
- token_grad: bfloat16 [4096, 2048], P(('dp', 'expert'))
- route_grad: float32 [4096, 2], P(('dp', 'expert'))
- gate_grad: bfloat16 [8, 2048, 384], P('expert', 'dp')
- up_grad: bfloat16 [8, 2048, 384], P('expert', 'dp')
- down_grad: bfloat16 [8, 2048, 384], P('expert', 'dp')
Inputs may be any that keep to these rules, and one draw needn't show every extreme that they name: `expert_ids`: each token names 2 different experts. Among the tokens of one device (aligned blocks of 128 tokens) no expert is named more than 48 times, and in some blocks one is named exactly 48 times.
All inputs are finite; a program needn't handle non-finite values.
Results may differ from a plain program's by a relative error of at most 0.0065.
Values may be sent and summed in bfloat16 or wider, within the bound.
A program may use at most 64 MiB of HBM per device.

v0:
```python
import functools

import jax
import jax.numpy as jnp
from jax import lax
from jax.experimental import pallas as pl
from jax.experimental.pallas import tpu as pltpu
from jax.sharding import PartitionSpec as P

BF16 = jnp.bfloat16
F32 = jnp.float32
CORES = 2
VMEM_MAX = 60 * 1024 * 1024


def slot_table(expert_ids, experts, capacity):
    flat = expert_ids.reshape(-1)
    count = flat.shape[0]
    same = flat[:, None] == flat[None, :]
    earlier = lax.broadcasted_iota(jnp.int32, (count, count), 0) > lax.broadcasted_iota(
        jnp.int32, (count, count), 1
    )
    rank = jnp.sum((same & earlier).astype(jnp.int32), axis=1)
    target = flat * capacity + rank
    columns = lax.broadcasted_iota(jnp.int32, (count, experts * capacity), 1)
    return (target[:, None] == columns).astype(jnp.bfloat16)


def contract_last(left, right):
    return lax.dot_general(
        left, right, (((1,), (1,)), ((), ())), preferred_element_type=jnp.float32
    )


def contract_first(left, right):
    return lax.dot_general(
        left, right, (((0,), (0,)), ((), ())), preferred_element_type=jnp.float32
    )


def expert_forward(rows, gate_w, up_w, down_w):
    gate = jnp.dot(rows, gate_w, preferred_element_type=jnp.float32)
    up = jnp.dot(rows, up_w, preferred_element_type=jnp.float32)
    sig = jax.nn.sigmoid(gate)
    hidden = (gate * sig * up).astype(jnp.bfloat16)
    expert_out = contract_last(hidden, down_w).astype(jnp.bfloat16)
    return (expert_out, (gate, up, sig, hidden))


def expert_backward(out_grad, saved, gate_w, up_w, down_w):
    gate, up, sig, hidden = saved
    hidden_grad = jnp.dot(out_grad, down_w, preferred_element_type=jnp.float32)
    gate_term = (hidden_grad * up * sig * (1.0 + gate * (1.0 - sig))).astype(jnp.bfloat16)
    up_term = (hidden_grad * gate * sig).astype(jnp.bfloat16)
    slot_grad = (contract_last(gate_term, gate_w) + contract_last(up_term, up_w)).astype(
        jnp.bfloat16
    )
    return (slot_grad, gate_term, up_term)


def weight_grads(rows, out_grad, gate_term, up_term, hidden):
    part_rows, part_grad = (
        lax.all_to_all(rows, "dp", split_axis=1, concat_axis=0, tiled=True),
        lax.all_to_all(out_grad, "dp", split_axis=1, concat_axis=0, tiled=True),
    )
    all_gate, all_up, all_hidden = (
        lax.all_gather(gate_term, "dp", axis=0, tiled=True),
        lax.all_gather(up_term, "dp", axis=0, tiled=True),
        lax.all_gather(hidden, "dp", axis=0, tiled=True),
    )
    down_g = contract_first(part_grad, all_hidden).astype(jnp.bfloat16)
    gate_g = contract_first(part_rows, all_gate).astype(jnp.bfloat16)
    up_g = contract_first(part_rows, all_up).astype(jnp.bfloat16)
    return (gate_g, up_g, down_g)


def body(tokens, expert_ids, route_weights, w_gate, w_up, w_down, grad_out):
    local = w_gate.shape[0]
    groups = lax.axis_size("expert")
    experts = local * groups
    count = tokens.shape[0]
    top = expert_ids.shape[1]
    width = tokens.shape[1]
    capacity = max(2, (3 * count * top + 2 * experts - 1) // (2 * experts))
    table = slot_table(expert_ids, experts, capacity)
    per_token = jnp.sum(table.reshape(count, top, experts * capacity), axis=1)
    send_rows = jnp.dot(per_token.T, tokens, preferred_element_type=jnp.float32)
    send_rows = send_rows.astype(jnp.bfloat16).reshape(experts, capacity, width)
    weighted = (route_weights[:, :, None] * grad_out.astype(jnp.float32)[:, None, :]).astype(
        jnp.bfloat16
    )
    send_grad = jnp.dot(
        table.T, weighted.reshape(count * top, width), preferred_element_type=jnp.float32
    )
    send_grad = send_grad.astype(jnp.bfloat16).reshape(experts, capacity, width)
    full_gate, full_up, full_down = (
        lax.all_gather(w_gate, "dp", axis=1, tiled=True),
        lax.all_gather(w_up, "dp", axis=1, tiled=True),
        lax.all_gather(w_down, "dp", axis=1, tiled=True),
    )
    received = lax.all_to_all(send_rows, "expert", split_axis=0, concat_axis=0, tiled=True)
    shaped = received.reshape(groups, local, capacity, width)
    saves = []
    inputs = []
    slot_expert = 0
    rows = shaped[:, slot_expert].reshape(groups * capacity, width)
    expert_out, saved = expert_forward(
        rows, full_gate[slot_expert], full_up[slot_expert], full_down[slot_expert]
    )
    outs = expert_out.reshape(groups, 1, capacity, width)
    saves.append(saved)
    inputs.append(rows)
    expert_outs, saves, inputs = (outs.reshape(experts, capacity, width), saves, inputs)
    back_out = lax.all_to_all(expert_outs, "expert", split_axis=0, concat_axis=0, tiled=True)
    received_grad = lax.all_to_all(send_grad, "expert", split_axis=0, concat_axis=0, tiled=True)
    shaped = received_grad.reshape(groups, local, capacity, width)
    slot_expert = 0
    out_grad = shaped[:, slot_expert].reshape(groups * capacity, width)
    slot_grad, gate_term, up_term = expert_backward(
        out_grad,
        saves[slot_expert],
        full_gate[slot_expert],
        full_up[slot_expert],
        full_down[slot_expert],
    )
    grads_in = slot_grad.reshape(groups, 1, capacity, width)
    gate_g, up_g, down_g = weight_grads(
        inputs[slot_expert], out_grad, gate_term, up_term, saves[slot_expert][3]
    )
    gate_list = [gate_g]
    up_list = [up_g]
    down_list = [down_g]
    slot_grads = grads_in.reshape(experts, capacity, width)
    gate_grad = jnp.stack(gate_list)
    up_grad = jnp.stack(up_list)
    down_grad = jnp.stack(down_list)
    back_grad = lax.all_to_all(slot_grads, "expert", split_axis=0, concat_axis=0, tiled=True)
    out_slots = jnp.dot(
        table, back_out.reshape(experts * capacity, width), preferred_element_type=jnp.float32
    )
    out_slots = out_slots.reshape(count, top, width)
    layer_out = jnp.sum(route_weights[:, :, None] * out_slots, axis=1).astype(jnp.bfloat16)
    route_grad = jnp.sum(grad_out.astype(jnp.float32)[:, None, :] * out_slots, axis=2)
    grad_slots = jnp.dot(
        table, back_grad.reshape(experts * capacity, width), preferred_element_type=jnp.float32
    )
    token_grad = jnp.sum(grad_slots.reshape(count, top, width), axis=1).astype(jnp.bfloat16)
    return (layer_out, token_grad, route_grad, gate_grad, up_grad, down_grad)


def pad16(n):
    return (n + 15) // 16 * 16


def prefix_count(member):
    t = member.shape[1]
    before = lax.broadcasted_iota(jnp.int32, (t, t), 0) < lax.broadcasted_iota(jnp.int32, (t, t), 1)
    return jnp.sum(member[:, :, None] * before.astype(F32)[None], axis=1)


def route_tables(expert_ids, route_weights, groups):
    count, top = expert_ids.shape
    stages = groups // CORES
    chip = lax.axis_index("expert") // CORES
    lanes = lax.broadcasted_iota(jnp.int32, (count,), 0)
    experts = lax.broadcasted_iota(jnp.int32, (groups, count), 0)
    member = jnp.zeros((groups, count), F32)
    weight = jnp.zeros((groups, count), F32)
    for k in range(top):
        hit = (expert_ids[:, k][None, :] == experts).astype(F32)
        member = member + hit
        weight = weight + hit * route_weights[:, k][None, :]
    slot = jnp.where(member > 0, prefix_count(member), -1.0)

    def position(first):
        key = jnp.where(first, lanes, lanes + count)
        return jnp.sum((key[:, None] < key[None, :]).astype(F32), axis=0)

    pos_up = position(jnp.any(expert_ids // CORES == stages - 1, axis=1))
    pos_down = position(jnp.any(expert_ids // CORES == 0, axis=1))
    dest = lax.broadcasted_iota(jnp.int32, (groups, 1), 0) // CORES
    pos = jnp.where(dest >= chip, pos_up[None, :], pos_down[None, :])
    pick = (pos[:, None, :] == lanes.astype(F32)[None, :, None]).astype(F32)
    slot_rows = jnp.sum(pick * slot[:, None, :], axis=2)
    weight_rows = jnp.sum(pick * weight[:, None, :], axis=2)
    swap = lambda a: a.reshape(stages, CORES, count)[:, ::-1].reshape(groups, count)
    zero = jnp.zeros_like(slot)
    meta = jnp.stack(
        [slot_rows, weight_rows, swap(slot_rows), slot, swap(slot), zero, zero, zero], axis=1
    )
    order = jnp.stack([pos_up, pos_down] + [jnp.zeros_like(pos_up)] * 6, axis=0)
    return meta, order


def one_hot(row, height):
    rows = lax.broadcasted_iota(jnp.int32, (height, row.shape[1]), 0).astype(F32)
    return (rows == row).astype(F32)


def choose(index, values):
    result = jnp.int32(values[0])
    for i in range(1, len(values)):
        result = jnp.where(index == i, jnp.int32(values[i]), result)
    return result


def visit_order(chip, stages):
    near = [s for d in range(stages) for s in ((chip - d, chip + d) if d else (chip,))]
    return [s for s in near if 0 <= s < stages]


def moe_kernel(
    groups, ndp, cap, edge,
    tok_ref, grad_ref, meta_ref, order_ref, wg_ref, wu_ref, wd_ref,
    out_ref, tgrad_ref, route_ref, gg_ref, ug_ref, dg_ref,
    blocks, own_down, metas, xr, gr, ogr, wr, wfull, y, partner, ret_in, ret_down, ret_out,
    grad_send, grad_own, grad_recv, route_out, route_in,
    in_send, in_recv, meta_send, meta_recv, w_send, w_recv, pc_send, pc_recv,
    ret_send, ret_recv, retd_recv, route_send, route_recv, gr_send, gr_recv,
):
    stages = groups // CORES
    count, width = tok_ref.shape
    part, ff = wg_ref.shape
    me = lax.axis_index("expert")
    dp = lax.axis_index("dp")
    chip, core = me // CORES, me % CORES
    mate = chip * CORES + (1 - core)
    at_edge = (chip == 0) | (chip == stages - 1)
    pending = []

    def copy(src, dst, ssem, rsem, where):
        return pltpu.make_async_remote_copy(
            src_ref=src, dst_ref=dst, send_sem=ssem, recv_sem=rsem,
            device_id=where, device_id_type=pl.DeviceIdType.MESH,
        )

    def send(cond, *args):
        if cond is None:
            copy(*args).start()
        else:
            pl.when(cond)(lambda: copy(*args).start())
        pending.append((cond, args))

    def send_rows(cond, short, src, dst, ssem, rsem, where):
        if edge == count:
            send(cond, src, dst, ssem, rsem, where)
            return
        full = jnp.logical_not(short)
        if cond is not None:
            short, full = cond & short, cond & full
        cut = pl.ds(0, edge)
        send(full, src, dst, ssem, rsem, where)
        send(short, src.at[cut], dst.at[cut], ssem, rsem, where)

    def wait_rows(cond, short, dst, sem):
        def one(c, ref):
            pl.when(c)(lambda: copy(ref, ref, sem, sem, {"expert": mate}).wait_recv())

        if edge == count:
            one(cond, dst)
            return
        one(cond & jnp.logical_not(short), dst)
        one(cond & short, dst.at[pl.ds(0, edge)])

    yes = chip >= 0
    if edge < count:
        rest = pl.ds(edge, count - edge)
        empty = jnp.zeros((count - edge, width), BF16)
        for t in range(2):
            for s in range(stages):
                blocks[0, t, s, rest] = empty
                blocks[1, t, s, rest] = empty
                ret_in[t, s, rest] = empty
            ret_down[t, rest] = empty
    for t in range(2):
        @pl.when(chip == stages - 1)
        def _():
            ret_in[t, chip] = jnp.zeros((count, width), BF16)

        @pl.when(chip == 0)
        def _():
            ret_down[t] = jnp.zeros((count, width), BF16)

    up_hot = one_hot(order_ref[0:1, :], count)
    down_hot = one_hot(order_ref[1:2, :], count)
    for t, ref in enumerate((tok_ref, grad_ref)):
        value = ref[...]
        blocks[0, t, chip] = jnp.dot(up_hot.astype(BF16), value, preferred_element_type=F32).astype(BF16)
        own_down[t] = jnp.dot(down_hot.astype(BF16), value, preferred_element_type=F32).astype(BF16)
    metas[me] = meta_ref[me]

    barrier = pltpu.get_barrier_semaphore()
    for off in range(1, groups):
        pl.semaphore_signal(barrier, inc=1, device_id={"expert": (me + off) % groups},
                            device_id_type=pl.DeviceIdType.MESH)
    for off in range(1, ndp):
        pl.semaphore_signal(barrier, inc=1, device_id={"dp": (dp + off) % ndp},
                            device_id_type=pl.DeviceIdType.MESH)
    pl.semaphore_wait(barrier, groups + ndp - 2)

    for off in range(1, groups):
        other = (me + off) % groups
        send(None, meta_ref.at[other], metas.at[me], meta_send.at[off - 1], meta_recv.at[off - 1],
             {"expert": other})
    has_up, has_down = chip < stages - 1, chip > 0
    up_dev, down_dev = {"expert": me + CORES}, {"expert": me - CORES}
    for t in range(2):
        send_rows(has_up, chip + 1 == stages - 1, blocks.at[0, t, chip], blocks.at[0, t, chip],
                  in_send.at[t, 0, 0], in_recv.at[0, t, chip], up_dev)
        send_rows(has_down, chip - 1 == 0, own_down.at[t], blocks.at[0, t, chip],
                  in_send.at[t, 0, 1], in_recv.at[0, t, chip], down_dev)
        send(None, blocks.at[0, t, chip], blocks.at[1, t, chip],
             in_send.at[t, 0, 2], in_recv.at[1, t, chip], {"expert": mate})
    for i, ref in enumerate((wg_ref, wu_ref, wd_ref)):
        for off in range(1, ndp):
            send(None, ref, wfull.at[i, dp], w_send.at[i, off - 1], w_recv.at[i, off - 1],
                 {"dp": (dp + off) % ndp})
        wfull[i, dp] = ref[...]
    for off in range(1, groups):
        copy(meta_ref.at[0], metas.at[0], meta_send.at[off - 1], meta_recv.at[off - 1],
             {"expert": mate}).wait_recv()

    table = [visit_order(z, stages) for z in range(stages)]
    source = [choose(chip, [table[z][q] for z in range(stages)]) for q in range(stages)]

    def compact(q, r):
        s = source[q]
        origin = s * CORES + (core if r == 0 else 1 - core)
        tile = metas[origin]
        hot = one_hot(tile[0:1, :], cap)
        scale = jnp.sum(hot * tile[1:2, :], axis=1, keepdims=True)
        hot = hot.astype(BF16)
        rows = pl.ds((q * 2 + r) * cap, cap)
        xr[rows, :] = jnp.dot(hot, blocks[r, 0, s], preferred_element_type=F32).astype(BF16)
        g = jnp.dot(hot, blocks[r, 1, s], preferred_element_type=F32)
        gr[rows, :] = g.astype(BF16)
        ogr[rows, :] = (scale * g).astype(BF16)
        wr[rows, :] = jnp.broadcast_to(scale, (cap, 128))

    compact(0, 0)
    for q in range(stages):
        s = source[q]
        if q:
            rising = s < chip
            nxt = jnp.where(rising, chip + 1, chip - 1)
            more = (nxt >= 0) & (nxt < stages)
            for t in range(2):
                wait_rows(yes, at_edge, blocks.at[0, t, s], in_recv.at[0, t, s])
                send_rows(more, (nxt == 0) | (nxt == stages - 1), blocks.at[0, t, s],
                          blocks.at[0, t, s], in_send.at[t, q, 0], in_recv.at[0, t, s],
                          {"expert": nxt * CORES + core})
                send_rows(None, at_edge, blocks.at[0, t, s], blocks.at[1, t, s],
                          in_send.at[t, q, 2], in_recv.at[1, t, s], {"expert": mate})
            compact(q, 0)
        for t in range(2):
            if q:
                wait_rows(yes, at_edge, blocks.at[1, t, s], in_recv.at[1, t, s])
            else:
                wait_rows(yes, chip < 0, blocks.at[1, t, s], in_recv.at[1, t, s])
        compact(q, 1)

    for i in range(3):
        for off in range(1, ndp):
            copy(wfull.at[i, 0], wfull.at[i, 0], w_send.at[i, 0], w_recv.at[i, off - 1],
                 {"expert": mate}).wait_recv()

    def nt(a, b):
        return lax.dot_general(a, b, (((1,), (1,)), ((), ())), preferred_element_type=F32)

    def tn(a, b):
        return lax.dot_general(a, b, (((0,), (0,)), ((), ())), preferred_element_type=F32)

    def cut(j):
        return pl.ds(j * part, part)

    total = xr.shape[0]
    gate = jnp.zeros((total, ff), F32)
    up = jnp.zeros((total, ff), F32)
    hg = jnp.zeros((total, ff), F32)
    for j in range(ndp):
        gate += jnp.dot(xr[:, cut(j)], wfull[0, j], preferred_element_type=F32)
        up += jnp.dot(xr[:, cut(j)], wfull[1, j], preferred_element_type=F32)
        hg += jnp.dot(ogr[:, cut(j)], wfull[2, j], preferred_element_type=F32)
    sig = jax.nn.sigmoid(gate)
    hidden = (gate * sig * up).astype(BF16)
    gt = (hg * up * sig * (1.0 + gate * (1.0 - sig))).astype(BF16)
    ut = (hg * gate * sig).astype(BF16)
    scale = wr[:, 0:1]
    dots = jnp.zeros((total, 1), F32)
    def to_mate(t):
        for q in reversed(range(stages)):
            send(None, y.at[t, pl.ds((q * 2 + 1) * cap, cap)], partner.at[t, q],
                 pc_send.at[t, q], pc_recv.at[t, q], {"expert": mate})

    for j in range(ndp):
        eo = nt(hidden, wfull[2, j]).astype(BF16).astype(F32)
        y[0, :, cut(j)] = (scale * eo).astype(BF16)
        dots += jnp.sum(gr[:, cut(j)].astype(F32) * eo, axis=1, keepdims=True)
    to_mate(0)
    for j in range(ndp):
        y[1, :, cut(j)] = (nt(gt, wfull[0, j]) + nt(ut, wfull[1, j])).astype(BF16)
    to_mate(1)

    both = jnp.concatenate([gt, ut], axis=1)

    def weight_slice(off):
        j = (dp + off) % ndp
        cols = pl.ds(pl.multiple_of(j * part, part), part)
        gu = tn(xr[:, cols], both)
        return gu[:, :ff], gu[:, ff:], tn(ogr[:, cols], hidden)

    def weight_part(off):
        for i, value in enumerate(weight_slice(off)):
            grad_send[i, off - 1] = value.astype(BF16)
        for i in range(3):
            send(None, grad_send.at[i, off - 1], grad_recv.at[i, off - 1], gr_send.at[i, off - 1],
                 gr_recv.at[i, off - 1], {"dp": (dp + off) % ndp})

    def expand(q, t, row_own, row_mate):
        tile = metas[source[q] * CORES + core]
        own = one_hot(tile[row_own:row_own + 1, :], cap).astype(BF16)
        other = one_hot(tile[row_mate:row_mate + 1, :], cap).astype(BF16)
        return tn(own, y[t, pl.ds(q * 2 * cap, cap), :]) + tn(other, partner[t, q])

    def give_back(q, ends):
        s = source[q]
        rising = s > chip
        nxt = jnp.where(rising, chip + 1, chip - 1)
        back = jnp.where(rising, chip - 1, chip + 1)
        where = {"expert": nxt * CORES + core}
        here = at_edge if ends else jnp.logical_not(at_edge)
        for t in range(2):
            pl.when(here)(lambda t=t: copy(
                partner.at[t, q], partner.at[t, q], pc_send.at[t, q], pc_recv.at[t, q],
                {"expert": mate}).wait_recv())
            if not ends:
                wait_rows(here, (back == 0) | (back == stages - 1), ret_in.at[t, s],
                          ret_recv.at[t, s])

            @pl.when(here)
            def _():
                value = expand(q, t, 0, 2)
                if not ends:
                    value = value + ret_in[t, s].astype(F32)
                ret_out[t, q] = value.astype(BF16)

            arrives = rising & (nxt == s)
            rows = pl.ds(0, edge) if ends else pl.ds(0, count)
            send(here & arrives, ret_out.at[t, q, rows], ret_down.at[t, rows], ret_send.at[t, q],
                 retd_recv.at[t], where)
            send(here & jnp.logical_not(arrives), ret_out.at[t, q, rows], ret_in.at[t, s, rows],
                 ret_send.at[t, q], ret_recv.at[t, s], where)

    for q in reversed(range(1, stages)):
        give_back(q, True)
    for off in range(1, ndp):
        weight_part(off)
    for q in reversed(range(1, stages)):
        give_back(q, False)

    for q in range(stages):
        for r in range(2):
            origin = source[q] * CORES + (core if r == 0 else 1 - core)
            hot = one_hot(metas[origin][3:4, :], cap)
            part_dots = dots[(q * 2 + r) * cap:(q * 2 + r + 1) * cap, :]
            line = jnp.sum(hot * part_dots, axis=0, keepdims=True)
            route_out[origin] = jnp.broadcast_to(line, (8, count))
    for off in range(1, groups):
        other = (me + off) % groups
        send(None, route_out.at[other], route_in.at[me], route_send.at[off - 1],
             route_recv.at[off - 1], {"expert": other})
    route_in[me] = route_out[me]

    own = weight_slice(0)
    for i in range(3):
        grad_own[i] = own[i]

    for t, ref in enumerate((out_ref, tgrad_ref)):
        copy(partner.at[t, 0], partner.at[t, 0], pc_send.at[t, 0], pc_recv.at[t, 0],
             {"expert": mate}).wait_recv()
        value = expand(0, t, 3, 4)
        wait_rows(has_up, chip + 1 == stages - 1, ret_in.at[t, chip], ret_recv.at[t, chip])
        wait_rows(has_down, chip - 1 == 0, ret_down.at[t], retd_recv.at[t])
        value += tn(up_hot.astype(BF16), ret_in[t, chip]) + tn(down_hot.astype(BF16), ret_down[t])
        ref[...] = value.astype(BF16)

    for off in range(1, groups):
        copy(route_out.at[0], route_in.at[0], route_send.at[off - 1], route_recv.at[off - 1],
             {"expert": mate}).wait_recv()
    route_ref[...] = route_in[...]
    for i, ref in enumerate((gg_ref, ug_ref, dg_ref)):
        value = grad_own[i]
        for off in range(1, ndp):
            copy(grad_recv.at[i, off - 1], grad_recv.at[i, off - 1], gr_send.at[i, off - 1],
                 gr_recv.at[i, off - 1], {"expert": mate}).wait_recv()
            value += grad_recv[i, off - 1].astype(F32)
        ref[...] = value.astype(BF16)
    for cond, args in pending:
        if cond is None:
            copy(*args).wait_send()
        else:
            pl.when(cond)(lambda args=args: copy(*args).wait_send())


def kernel_scratch(groups, ndp, cap, count, width, part, ff):
    stages = groups // CORES
    rows = groups * cap
    shapes = [
        ((2, 2, stages, count, width), BF16),
        ((2, count, width), BF16),
        ((groups, 8, count), F32),
        ((rows, width), BF16),
        ((rows, width), BF16),
        ((rows, width), BF16),
        ((rows, 128), F32),
        ((3, ndp, part, ff), BF16),
        ((2, rows, width), BF16),
        ((2, stages, cap, width), BF16),
        ((2, stages, count, width), BF16),
        ((2, count, width), BF16),
        ((2, stages, count, width), BF16),
        ((3, ndp - 1, part, ff), BF16),
        ((3, part, ff), F32),
        ((3, ndp - 1, part, ff), BF16),
        ((groups, 8, count), F32),
        ((groups, 8, count), F32),
    ]
    sems = [
        (2, stages, 3), (2, 2, stages), (groups - 1,), (groups - 1,), (3, ndp - 1), (3, ndp - 1),
        (2, stages), (2, stages), (2, stages), (2, stages), (2,), (groups - 1,), (groups - 1,),
        (3, ndp - 1), (3, ndp - 1),
    ]
    return shapes, sems


def scratch_bytes(shapes):
    total = 0
    for shape, dtype in shapes:
        size = jnp.dtype(dtype).itemsize
        for n in shape:
            size *= n
        total += size
    return total


def slot_capacity(count, top, experts):
    return max(2, (3 * count * top + 2 * experts - 1) // (2 * experts))


def line_body(groups, ndp, tokens, expert_ids, route_weights, w_gate, w_up, w_down, grad_out):
    count, width = tokens.shape
    _, part, ff = w_gate.shape
    top = expert_ids.shape[1]
    slots = slot_capacity(count, top, groups)
    cap = pad16(slots)
    edge = min(count, pad16(CORES * slots))
    meta, order = route_tables(expert_ids, route_weights, groups)
    shapes, sems = kernel_scratch(groups, ndp, cap, count, width, part, ff)
    vmem = pl.BlockSpec(memory_space=pltpu.VMEM)
    layer_out, token_grad, route, gate_g, up_g, down_g = pl.pallas_call(
        functools.partial(moe_kernel, groups, ndp, cap, edge),
        out_shape=(
            jax.ShapeDtypeStruct((count, width), BF16),
            jax.ShapeDtypeStruct((count, width), BF16),
            jax.ShapeDtypeStruct((groups, 8, count), F32),
            jax.ShapeDtypeStruct((part, ff), BF16),
            jax.ShapeDtypeStruct((part, ff), BF16),
            jax.ShapeDtypeStruct((part, ff), BF16),
        ),
        in_specs=[vmem] * 7,
        out_specs=(vmem,) * 6,
        scratch_shapes=[pltpu.VMEM(s, d) for s, d in shapes]
        + [pltpu.SemaphoreType.DMA(s) for s in sems],
        compiler_params=pltpu.CompilerParams(
            collective_id=0, has_side_effects=True, vmem_limit_bytes=VMEM_MAX
        ),
    )(tokens, grad_out, meta, order, w_gate[0], w_up[0], w_down[0])
    experts = lax.broadcasted_iota(jnp.int32, (groups, count, top), 0)
    mine = (expert_ids[None] == experts).astype(F32)
    route_grad = jnp.sum(mine * route[:, 0, :, None], axis=0)
    return layer_out, token_grad, route_grad, gate_g[None], up_g[None], down_g[None]


def pick_body(groups, ndp, *args):
    tokens, expert_ids, _, w_gate = args[:4]
    count, width = tokens.shape
    local, part, ff = w_gate.shape
    if local == 1 and groups % CORES == 0 and groups > CORES and ndp > 1:
        cap = pad16(slot_capacity(count, expert_ids.shape[1], groups))
        shapes, _ = kernel_scratch(groups, ndp, cap, count, width, part, ff)
        if scratch_bytes(shapes) < VMEM_MAX * 3 // 4:
            return line_body(groups, ndp, *args)
    return body(*args)


def solution(mesh):
    in_specs = (
        P(("dp", "expert"), None),
        P(("dp", "expert"), None),
        P(("dp", "expert"), None),
        P("expert", "dp", None),
        P("expert", "dp", None),
        P("expert", "dp", None),
        P(("dp", "expert"), None),
    )
    out_specs = (
        P(("dp", "expert"), None),
        P(("dp", "expert"), None),
        P(("dp", "expert"), None),
        P("expert", "dp", None),
        P("expert", "dp", None),
        P("expert", "dp", None),
    )
    step = functools.partial(pick_body, mesh.shape["expert"], mesh.shape["dp"])
    return jax.shard_map(step, mesh=mesh, in_specs=in_specs, out_specs=out_specs, check_vma=False)
```

profile of v0, /device:TPU:0, one launch (start us, length us, event | category | flops | bytes accessed | tf_op | source)
XLA Modules:
  0.0 155.6 jit_solution(12571362085017857453)
XLA Ops:
  0.7 0.1 pad.2.clone
  0.7 0.1 pad.3.clone
  0.8 0.0 copy-start.5
  0.8 0.7 copy-done.5
  1.5 0.0 copy-start.4
  1.5 0.7 copy-done.4
  2.2 0.1 convert_reduce_fusion
  2.3 0.1 convert_reduce_fusion.1
  2.4 0.7 maximum_maximum_fusion.order_ref
  3.1 0.1 broadcast_select_fusion
  3.2 0.2 multiply_reduce_fusion
  3.4 0.1 compare_select_fusion.3
  3.5 0.4 fusion.1
  4.0 0.7 stack.27.meta_ref
  4.7 143.4 %shard_map.118 = (bf16[128,2048]{1,0:T(8,128)(2,1)}, bf16[128,2048]{1,0:T(8,128)(2,1)}, f32[8,8,128]{2,1,0:T(8,128)}, bf16[512,384]{1,0:T(8,128)(2,1)}, bf16[512...) custom-call(bf16[128,2048]{1,0:T(8,128)(2,1)} %tok_ref.1, bf16[128,2048]{1,0:T(8,128)(2,1)} %grad_ref.1, ...), custom_call_target="tpu_custom_call" | custom-call | tf_op jit(solution)/shard_map/pallas_call | solution.py:560
  148.1 0.8 slice.19
  148.8 0.6 select_reduce_fusion
  149.4 0.0 copy-start
  149.4 1.9 %copy.19 = bf16[128,2048]{1,0:T(8,128)(2,1)} copy(bf16[128,2048]{1,0:T(8,128)(2,1)} %get-tuple-element.36) | data formatting | bytes 1048576
  151.3 0.0 copy-done
  151.4 0.0 copy-start.3
  151.4 0.8 copy.20
  152.1 0.4 copy-done.3
  152.5 0.0 copy-start.2
  152.5 0.7 copy.21
  153.3 0.4 copy-done.2
  153.7 0.0 copy-start.1
  153.7 0.7 copy.22
  154.4 0.4 copy-done.1
  154.8 0.7 copy.23
  (17 shorter events, 0.2 us)
Async XLA Ops:
  0.8 0.7 copy-start.5
  1.5 0.7 copy-start.4
  149.4 1.9 %copy-start = (bf16[128,2048]{1,0:T(8,128)(2,1)S(1)}, bf16[128,2048]{1,0:T(8,128)(2,1)}, u32[]{:S(2)}) copy-start(bf16[128,2048]{1,0:T(8,128)(2,1)} %get-tuple-element.37) | copy-start | bytes 1572868
  151.4 1.2 copy-start.3
  152.5 1.1 copy-start.2
  153.7 1.1 copy-start.1
where the time goes:
time: 156 us
  Pallas kernels  143 us (92%)
  local copies, waits for them, and re-layouts  9.15 us (6%)
  other arithmetic  2.32 us (1%)
    pallas_call x1, Pallas kernels, line_body(): pl.pallas_call(functools.partial(moe_kernel, groups, ndp, cap, edge), out...  143 us
    unnamed x17, local copies, waits for them, and re-layouts  7.5 us

commit v1 on v0

--- a/solution.py
+++ b/solution.py
@@ -205,27 +205,37 @@
 
 
 def visit_order(chip, stages):
-    near = [s for d in range(stages) for s in ((chip - d, chip + d) if d else (chip,))]
+    inner = -1 if 2 * chip >= stages else 1
+    near = [s for d in range(stages) for s in ((chip + d * inner, chip - d * inner) if d else (chip,))]
     return [s for s in near if 0 <= s < stages]
 
 
 def moe_kernel(
     groups, ndp, cap, edge,
-    tok_ref, grad_ref, meta_ref, order_ref, wg_ref, wu_ref, wd_ref,
-    out_ref, tgrad_ref, route_ref, gg_ref, ug_ref, dg_ref,
-    blocks, own_down, metas, xr, gr, ogr, wr, wfull, y, partner, ret_in, ret_down, ret_out,
-    grad_send, grad_own, grad_recv, route_out, route_in,
+    tok_hbm, grad_hbm, meta_ref, order_ref, wg_hbm, wu_hbm, wd_hbm,
+    out_hbm, tgrad_hbm, route_ref, gg_hbm, ug_hbm, dg_hbm,
+    tok, grad, blocks, own_down, metas, xr, gr, wr, wgu, wd, yy, ym, ret_in, ret_down, ret_out,
+    fa, fb, hid, hs, both, dots, gs, gs2, grx, keep, own, gout, route_out, route_in,
     in_send, in_recv, meta_send, meta_recv, w_send, w_recv, pc_send, pc_recv,
-    ret_send, ret_recv, retd_recv, route_send, route_recv, gr_send, gr_recv,
+    ret_send, ret_recv, retd_recv, route_send, route_recv, gr_send, gr_recv, load_sem, store_sem,
 ):
     stages = groups // CORES
-    count, width = tok_ref.shape
-    part, ff = wg_ref.shape
+    count, width = tok.shape
+    part, ff = gout.shape[1:]
+    half, hp = count // 2, part // 2
     me = lax.axis_index("expert")
     dp = lax.axis_index("dp")
     chip, core = me // CORES, me % CORES
     mate = chip * CORES + (1 - core)
+    px, py = dp % 2, dp // 2
+    xn, yn, dg = py * 2 + (1 - px), (1 - py) * 2 + px, (1 - py) * 2 + (1 - px)
+    to_mate, to_x, to_y = {"expert": mate}, {"dp": xn}, {"dp": yn}
     at_edge = (chip == 0) | (chip == stages - 1)
+    inside = jnp.logical_not(at_edge)
+    has_up, has_down = chip < stages - 1, chip > 0
+    up_dev, down_dev = {"expert": me + CORES}, {"expert": me - CORES}
+    low = 2 * chip < stages
+    yes = chip >= 0
     pending = []
 
     def copy(src, dst, ssem, rsem, where):
@@ -241,28 +251,54 @@
             pl.when(cond)(lambda: copy(*args).start())
         pending.append((cond, args))
 
-    def send_rows(cond, short, src, dst, ssem, rsem, where):
-        if edge == count:
-            send(cond, src, dst, ssem, rsem, where)
+    def landed(ref, sem):
+        copy(ref, ref, sem, sem, to_mate).wait_recv()
+
+    def rows_of(c, short):
+        end = half if c == 0 else (edge if short else count)
+        return pl.ds(c * half, end - c * half)
+
+    def send_rows(cond, short, c, src, dst, ssem, rsem, where):
+        if c == 0 or edge == count:
+            send(cond, src.at[rows_of(c, False)], dst.at[rows_of(c, False)], ssem, rsem, where)
             return
         full = jnp.logical_not(short)
         if cond is not None:
             short, full = cond & short, cond & full
-        cut = pl.ds(0, edge)
-        send(full, src, dst, ssem, rsem, where)
-        send(short, src.at[cut], dst.at[cut], ssem, rsem, where)
-
-    def wait_rows(cond, short, dst, sem):
-        def one(c, ref):
-            pl.when(c)(lambda: copy(ref, ref, sem, sem, {"expert": mate}).wait_recv())
-
-        if edge == count:
-            one(cond, dst)
+        for when, cut in ((full, rows_of(c, False)), (short, rows_of(c, True))):
+            send(when, src.at[cut], dst.at[cut], ssem, rsem, where)
+
+    def wait_rows(cond, short, c, dst, sem):
+        if c == 0 or edge == count:
+            pl.when(cond)(lambda: landed(dst.at[rows_of(c, False)], sem))
             return
-        one(cond & jnp.logical_not(short), dst)
-        one(cond & short, dst.at[pl.ds(0, edge)])
-
-    yes = chip >= 0
+        pl.when(cond & jnp.logical_not(short))(lambda: landed(dst.at[rows_of(c, False)], sem))
+        pl.when(cond & short)(lambda: landed(dst.at[rows_of(c, True)], sem))
+
+    def nt(a, b):
+        return lax.dot_general(a, b, (((1,), (1,)), ((), ())), preferred_element_type=F32)
+
+    def tn(a, b):
+        return lax.dot_general(a, b, (((0,), (0,)), ((), ())), preferred_element_type=F32)
+
+    def nn(a, b):
+        return jnp.dot(a, b, preferred_element_type=F32)
+
+    gate_cols, up_cols = pl.ds(0, ff), pl.ds(ff, ff)
+
+    def weight(i, j):
+        return wd.at[j] if i == 2 else wgu.at[j, :, gate_cols if i == 0 else up_cols]
+
+    loads = [
+        pltpu.make_async_copy(src, dst, load_sem.at[n])
+        for n, (src, dst) in enumerate((
+            (tok_hbm, tok), (wg_hbm, weight(0, dp)), (wu_hbm, weight(1, dp)), (grad_hbm, grad),
+            (wd_hbm, weight(2, dp)),
+        ))
+    ]
+    for load in loads:
+        load.start()
+
     if edge < count:
         rest = pl.ds(edge, count - edge)
         empty = jnp.zeros((count - edge, width), BF16)
@@ -281,13 +317,17 @@
         def _():
             ret_down[t] = jnp.zeros((count, width), BF16)
 
-    up_hot = one_hot(order_ref[0:1, :], count)
-    down_hot = one_hot(order_ref[1:2, :], count)
-    for t, ref in enumerate((tok_ref, grad_ref)):
-        value = ref[...]
-        blocks[0, t, chip] = jnp.dot(up_hot.astype(BF16), value, preferred_element_type=F32).astype(BF16)
-        own_down[t] = jnp.dot(down_hot.astype(BF16), value, preferred_element_type=F32).astype(BF16)
+    up_hot = one_hot(order_ref[0:1, :], count).astype(BF16)
+    down_hot = one_hot(order_ref[1:2, :], count).astype(BF16)
     metas[me] = meta_ref[me]
+
+    def arrange(t):
+        value = (tok, grad)[t][...]
+        blocks[0, t, chip] = nn(up_hot, value).astype(BF16)
+        own_down[t] = nn(down_hot, value).astype(BF16)
+
+    loads[0].wait()
+    arrange(0)
 
     barrier = pltpu.get_barrier_semaphore()
     for off in range(1, groups):
@@ -298,171 +338,259 @@
                             device_id_type=pl.DeviceIdType.MESH)
     pl.semaphore_wait(barrier, groups + ndp - 2)
 
+    def depart_up(t, cond):
+        for c in range(2):
+            send_rows(cond, chip + 1 == stages - 1, c, blocks.at[0, t, chip], blocks.at[0, t, chip],
+                      in_send.at[t, 0, 0, c], in_recv.at[0, t, chip, c], up_dev)
+
+    def depart_down(t, cond):
+        for c in range(2):
+            send_rows(cond, chip - 1 == 0, c, own_down.at[t], blocks.at[0, t, chip],
+                      in_send.at[t, 0, 1, c], in_recv.at[0, t, chip, c], down_dev)
+
+    def depart_mate(t):
+        send(None, blocks.at[0, t, chip], blocks.at[1, t, chip],
+             in_send.at[t, 0, 2, 0], in_recv.at[1, t, chip, 0], to_mate)
+
+    halves = (pl.ds(0, hp), pl.ds(hp, hp))
+
+    def weight_direct(i):
+        for n, (h, where) in enumerate(((0, to_x), (1, to_y), (1, to_x), (0, to_y))):
+            ref = weight(i, dp).at[halves[h]]
+            send(None, ref, ref, w_send.at[i, n], w_recv.at[i, n], where)
+
+    def weight_relay(i):
+        for n, (h, j, where) in enumerate(((0, xn, to_y), (1, yn, to_x))):
+            ref = weight(i, j).at[halves[h]]
+            landed(ref, w_recv.at[i, n])
+            send(None, ref, ref, w_send.at[i, 4 + n], w_recv.at[i, 4 + n], where)
+
+    def weight_rest(i):
+        for n, (h, j) in ((2, (1, xn)), (3, (0, yn)), (4, (0, dg)), (5, (1, dg))):
+            landed(weight(i, j).at[halves[h]], w_recv.at[i, n])
+
+    depart_up(0, has_up)
+    depart_down(0, has_down)
+    depart_mate(0)
     for off in range(1, groups):
         other = (me + off) % groups
         send(None, meta_ref.at[other], metas.at[me], meta_send.at[off - 1], meta_recv.at[off - 1],
              {"expert": other})
-    has_up, has_down = chip < stages - 1, chip > 0
-    up_dev, down_dev = {"expert": me + CORES}, {"expert": me - CORES}
-    for t in range(2):
-        send_rows(has_up, chip + 1 == stages - 1, blocks.at[0, t, chip], blocks.at[0, t, chip],
-                  in_send.at[t, 0, 0], in_recv.at[0, t, chip], up_dev)
-        send_rows(has_down, chip - 1 == 0, own_down.at[t], blocks.at[0, t, chip],
-                  in_send.at[t, 0, 1], in_recv.at[0, t, chip], down_dev)
-        send(None, blocks.at[0, t, chip], blocks.at[1, t, chip],
-             in_send.at[t, 0, 2], in_recv.at[1, t, chip], {"expert": mate})
-    for i, ref in enumerate((wg_ref, wu_ref, wd_ref)):
-        for off in range(1, ndp):
-            send(None, ref, wfull.at[i, dp], w_send.at[i, off - 1], w_recv.at[i, off - 1],
-                 {"dp": (dp + off) % ndp})
-        wfull[i, dp] = ref[...]
+    for i in range(2):
+        loads[1 + i].wait()
+        weight_direct(i)
+    loads[3].wait()
+    arrange(1)
+    depart_up(1, has_up & at_edge)
+    depart_down(1, has_down & at_edge)
+    depart_mate(1)
     for off in range(1, groups):
         copy(meta_ref.at[0], metas.at[0], meta_send.at[off - 1], meta_recv.at[off - 1],
-             {"expert": mate}).wait_recv()
+             to_mate).wait_recv()
 
     table = [visit_order(z, stages) for z in range(stages)]
     source = [choose(chip, [table[z][q] for z in range(stages)]) for q in range(stages)]
 
-    def compact(q, r):
+    def arrive(t, q, c):
         s = source[q]
-        origin = s * CORES + (core if r == 0 else 1 - core)
-        tile = metas[origin]
-        hot = one_hot(tile[0:1, :], cap)
-        scale = jnp.sum(hot * tile[1:2, :], axis=1, keepdims=True)
-        hot = hot.astype(BF16)
-        rows = pl.ds((q * 2 + r) * cap, cap)
-        xr[rows, :] = jnp.dot(hot, blocks[r, 0, s], preferred_element_type=F32).astype(BF16)
-        g = jnp.dot(hot, blocks[r, 1, s], preferred_element_type=F32)
-        gr[rows, :] = g.astype(BF16)
-        ogr[rows, :] = (scale * g).astype(BF16)
-        wr[rows, :] = jnp.broadcast_to(scale, (cap, 128))
+        nxt = jnp.where(s < chip, chip + 1, chip - 1)
+        more = (nxt >= 0) & (nxt < stages)
+        wait_rows(yes, at_edge, c, blocks.at[0, t, s], in_recv.at[0, t, s, c])
+        send_rows(more, (nxt == 0) | (nxt == stages - 1), c, blocks.at[0, t, s],
+                  blocks.at[0, t, s], in_send.at[t, q, 0, c], in_recv.at[0, t, s, c],
+                  {"expert": nxt * CORES + core})
+        send_rows(None, at_edge, c, blocks.at[0, t, s], blocks.at[1, t, s],
+                  in_send.at[t, q, 2, c], in_recv.at[1, t, s, c], to_mate)
+
+    def compact(t, q):
+        s = source[q]
+        for r in range(2):
+            if r == 1 and q == 0:
+                landed(blocks.at[1, t, s], in_recv.at[1, t, s, 0])
+            elif r == 1:
+                for c in range(2):
+                    wait_rows(yes, at_edge, c, blocks.at[1, t, s], in_recv.at[1, t, s, c])
+            tile = metas[s * CORES + (core if r == 0 else 1 - core)]
+            hot = one_hot(tile[0:1, :], cap)
+            rows = pl.ds((q * 2 + r) * cap, cap)
+            (xr, gr)[t][rows, :] = nn(hot.astype(BF16), blocks[r, t, s]).astype(BF16)
+            if t == 0:
+                scale = jnp.sum(hot * tile[1:2, :], axis=1, keepdims=True)
+                wr[rows, :] = jnp.broadcast_to(scale, (cap, 128))
 
     compact(0, 0)
-    for q in range(stages):
-        s = source[q]
-        if q:
-            rising = s < chip
-            nxt = jnp.where(rising, chip + 1, chip - 1)
-            more = (nxt >= 0) & (nxt < stages)
-            for t in range(2):
-                wait_rows(yes, at_edge, blocks.at[0, t, s], in_recv.at[0, t, s])
-                send_rows(more, (nxt == 0) | (nxt == stages - 1), blocks.at[0, t, s],
-                          blocks.at[0, t, s], in_send.at[t, q, 0], in_recv.at[0, t, s],
-                          {"expert": nxt * CORES + core})
-                send_rows(None, at_edge, blocks.at[0, t, s], blocks.at[1, t, s],
-                          in_send.at[t, q, 2], in_recv.at[1, t, s], {"expert": mate})
-            compact(q, 0)
-        for t in range(2):
-            if q:
-                wait_rows(yes, at_edge, blocks.at[1, t, s], in_recv.at[1, t, s])
-            else:
-                wait_rows(yes, chip < 0, blocks.at[1, t, s], in_recv.at[1, t, s])
-        compact(q, 1)
-
-    for i in range(3):
-        for off in range(1, ndp):
-            copy(wfull.at[i, 0], wfull.at[i, 0], w_send.at[i, 0], w_recv.at[i, off - 1],
-                 {"expert": mate}).wait_recv()
-
-    def nt(a, b):
-        return lax.dot_general(a, b, (((1,), (1,)), ((), ())), preferred_element_type=F32)
-
-    def tn(a, b):
-        return lax.dot_general(a, b, (((0,), (0,)), ((), ())), preferred_element_type=F32)
+    near = range(1, stages - 1)
+    last = stages - 1
+    for q in near:
+        arrive(0, q, 0)
+    for i in range(2):
+        weight_relay(i)
+    loads[4].wait()
+    weight_direct(2)
+    for q in near:
+        arrive(0, q, 1)
+    for q in near:
+        compact(0, q)
+    arrive(0, last, 0)
+    depart_up(1, inside & low)
+    depart_down(1, inside & jnp.logical_not(low))
+    arrive(0, last, 1)
+    depart_up(1, inside & jnp.logical_not(low))
+    depart_down(1, inside & low)
+    compact(0, last)
+    for i in range(2):
+        weight_rest(i)
 
     def cut(j):
         return pl.ds(j * part, part)
 
+    def cut_at(j):
+        return pl.ds(pl.multiple_of(j * part, part), part)
+
     total = xr.shape[0]
-    gate = jnp.zeros((total, ff), F32)
-    up = jnp.zeros((total, ff), F32)
-    hg = jnp.zeros((total, ff), F32)
+    gu = jnp.zeros((total, 2 * ff), F32)
     for j in range(ndp):
-        gate += jnp.dot(xr[:, cut(j)], wfull[0, j], preferred_element_type=F32)
-        up += jnp.dot(xr[:, cut(j)], wfull[1, j], preferred_element_type=F32)
-        hg += jnp.dot(ogr[:, cut(j)], wfull[2, j], preferred_element_type=F32)
+        gu += nn(xr[:, cut(j)], wgu[j])
+    gate, up = gu[:, :ff], gu[:, ff:]
     sig = jax.nn.sigmoid(gate)
-    hidden = (gate * sig * up).astype(BF16)
-    gt = (hg * up * sig * (1.0 + gate * (1.0 - sig))).astype(BF16)
-    ut = (hg * gate * sig).astype(BF16)
     scale = wr[:, 0:1]
-    dots = jnp.zeros((total, 1), F32)
-    def to_mate(t):
-        for q in reversed(range(stages)):
-            send(None, y.at[t, pl.ds((q * 2 + 1) * cap, cap)], partner.at[t, q],
-                 pc_send.at[t, q], pc_recv.at[t, q], {"expert": mate})
-
-    for j in range(ndp):
-        eo = nt(hidden, wfull[2, j]).astype(BF16).astype(F32)
-        y[0, :, cut(j)] = (scale * eo).astype(BF16)
-        dots += jnp.sum(gr[:, cut(j)].astype(F32) * eo, axis=1, keepdims=True)
-    to_mate(0)
-    for j in range(ndp):
-        y[1, :, cut(j)] = (nt(gt, wfull[0, j]) + nt(ut, wfull[1, j])).astype(BF16)
-    to_mate(1)
-
-    both = jnp.concatenate([gt, ut], axis=1)
-
-    def weight_slice(off):
-        j = (dp + off) % ndp
-        cols = pl.ds(pl.multiple_of(j * part, part), part)
-        gu = tn(xr[:, cols], both)
-        return gu[:, :ff], gu[:, ff:], tn(ogr[:, cols], hidden)
-
-    def weight_part(off):
-        for i, value in enumerate(weight_slice(off)):
-            grad_send[i, off - 1] = value.astype(BF16)
-        for i in range(3):
-            send(None, grad_send.at[i, off - 1], grad_recv.at[i, off - 1], gr_send.at[i, off - 1],
-                 gr_recv.at[i, off - 1], {"dp": (dp + off) % ndp})
-
-    def expand(q, t, row_own, row_mate):
+    gated = gate * sig
+    value = gated * up
+    hid[...] = value.astype(BF16)
+    hs[...] = (scale * value).astype(BF16)
+    fa[...] = scale * (up * sig * (1.0 + gate * (1.0 - sig)))
+    fb[...] = scale * gated
+
+    for q in near:
+        arrive(1, q, 0)
+    weight_relay(2)
+    for q in near:
+        arrive(1, q, 1)
+    for q in range(last):
+        compact(1, q)
+
+    def place(t, cols, value, qs):
+        for n, q in enumerate(qs):
+            yy[t, q, 0:cap, cols] = value[2 * n * cap:(2 * n + 1) * cap]
+            ym[t, q, :, cols] = value[(2 * n + 1) * cap:(2 * n + 2) * cap]
+
+    def pair(t, qs):
+        for q in reversed(qs):
+            send(None, ym.at[t, q], yy.at[t, q, pl.ds(cap, cap)], pc_send.at[t, q],
+                 pc_recv.at[t, q], to_mate)
+
+    everyone = range(stages)
+    for n, j in enumerate((dp, xn, yn, dg)):
+        if n == 1:
+            weight_rest(2)
+        place(0, cut_at(j), nt(hs[...], wd[j]).astype(BF16), everyone)
+    pair(0, everyone)
+
+    def expand(t, q, c, row_own, row_mate):
         tile = metas[source[q] * CORES + core]
-        own = one_hot(tile[row_own:row_own + 1, :], cap).astype(BF16)
-        other = one_hot(tile[row_mate:row_mate + 1, :], cap).astype(BF16)
-        return tn(own, y[t, pl.ds(q * 2 * cap, cap), :]) + tn(other, partner[t, q])
-
-    def give_back(q, ends):
+        hot = jnp.concatenate(
+            [one_hot(tile[row_own:row_own + 1, :], cap), one_hot(tile[row_mate:row_mate + 1, :], cap)],
+            axis=0).astype(BF16)
+        if c is not None:
+            hot = hot[:, c * half:(c + 1) * half]
+        return tn(hot, yy[t, q])
+
+    def give_back(t, q, ends):
         s = source[q]
         rising = s > chip
         nxt = jnp.where(rising, chip + 1, chip - 1)
         back = jnp.where(rising, chip - 1, chip + 1)
         where = {"expert": nxt * CORES + core}
-        here = at_edge if ends else jnp.logical_not(at_edge)
-        for t in range(2):
-            pl.when(here)(lambda t=t: copy(
-                partner.at[t, q], partner.at[t, q], pc_send.at[t, q], pc_recv.at[t, q],
-                {"expert": mate}).wait_recv())
+        here = at_edge if ends else inside
+        arrives = rising & (nxt == s)
+        pl.when(here)(lambda: landed(yy.at[t, q, pl.ds(cap, cap)], pc_recv.at[t, q]))
+        for c in range(2):
+            lines = pl.ds(c * half, half)
             if not ends:
-                wait_rows(here, (back == 0) | (back == stages - 1), ret_in.at[t, s],
-                          ret_recv.at[t, s])
+                wait_rows(here, (back == 0) | (back == stages - 1), c, ret_in.at[t, s],
+                          ret_recv.at[t, s, c])
 
             @pl.when(here)
             def _():
-                value = expand(q, t, 0, 2)
+                value = expand(t, q, c, 0, 2)
                 if not ends:
-                    value = value + ret_in[t, s].astype(F32)
-                ret_out[t, q] = value.astype(BF16)
-
-            arrives = rising & (nxt == s)
-            rows = pl.ds(0, edge) if ends else pl.ds(0, count)
-            send(here & arrives, ret_out.at[t, q, rows], ret_down.at[t, rows], ret_send.at[t, q],
-                 retd_recv.at[t], where)
+                    value = value + ret_in[t, s, lines].astype(F32)
+                ret_out[t, q, lines] = value.astype(BF16)
+
+            rows = rows_of(c, ends)
+            send(here & arrives, ret_out.at[t, q, rows], ret_down.at[t, rows], ret_send.at[t, q, c],
+                 retd_recv.at[t, c], where)
             send(here & jnp.logical_not(arrives), ret_out.at[t, q, rows], ret_in.at[t, s, rows],
-                 ret_send.at[t, q], ret_recv.at[t, s], where)
-
-    for q in reversed(range(1, stages)):
-        give_back(q, True)
-    for off in range(1, ndp):
-        weight_part(off)
-    for q in reversed(range(1, stages)):
-        give_back(q, False)
+                 ret_send.at[t, q, c], ret_recv.at[t, s, c], where)
+
+    def backward(qs):
+        rows = pl.ds(qs[0] * 2 * cap, len(qs) * 2 * cap)
+        hg = nn(gr[rows, cut(0)], wd[0])
+        for j in range(1, ndp):
+            hg += nn(gr[rows, cut(j)], wd[j])
+        both[rows, :ff] = (hg * fa[rows, :]).astype(BF16)
+        both[rows, ff:] = (hg * fb[rows, :]).astype(BF16)
+        line = jnp.sum(hg * hid[rows, :].astype(F32), axis=1, keepdims=True)
+        dots[rows, :] = jnp.broadcast_to(line, (line.shape[0], 128))
+        for j in range(ndp):
+            place(1, cut(j), nt(both[rows, :], wgu[j]).astype(BF16), qs)
+        pair(1, qs)
+
+    give_back(0, last, True)
+    for q in reversed(near):
+        if q > 1:
+            give_back(0, q, True)
+    arrive(1, last, 0)
+    backward(range(last))
+    arrive(1, last, 1)
+    compact(1, last)
+    backward(range(last, stages))
+
+    def weight_slice(j):
+        cols = cut_at(j)
+        return nn_t(xr, cols, both), nn_t(gr, cols, hs)
+
+    def nn_t(rows_ref, cols, ref):
+        return tn(rows_ref[:, cols], ref[...])
+
+    def pieces(value, down, h):
+        top = slice(h * hp, (h + 1) * hp)
+        return value[top, :ff], value[top, ff:], down[top]
+
+    def give_grad(k, h, values, where):
+        for i, v in enumerate(pieces(*values, h)):
+            gs[i, k] = v.astype(BF16)
+        for i in range(3):
+            send(None, gs.at[i, k], grx.at[i, k], gr_send.at[i, k], gr_recv.at[i, k], where)
+
+    def keep_grad(k, h, values):
+        for i, v in enumerate(pieces(*values, h)):
+            keep[i, k] = v
+
+    values = weight_slice(dg)
+    give_grad(0, 0, values, to_x)
+    give_grad(1, 1, values, to_y)
+    give_back(0, last, False)
+    give_back(1, last, True)
+    values = weight_slice(xn)
+    give_grad(2, 0, values, to_x)
+    keep_grad(1, 1, values)
+    values = weight_slice(yn)
+    give_grad(3, 1, values, to_y)
+    keep_grad(0, 0, values)
+    for q in near:
+        give_back(0, q, False)
+    for q in reversed(near):
+        if q > 1:
+            give_back(1, q, True)
+    for t in range(2):
+        give_back(t, 1, True)
 
     for q in range(stages):
         for r in range(2):
             origin = source[q] * CORES + (core if r == 0 else 1 - core)
             hot = one_hot(metas[origin][3:4, :], cap)
-            part_dots = dots[(q * 2 + r) * cap:(q * 2 + r + 1) * cap, :]
+            part_dots = dots[(q * 2 + r) * cap:(q * 2 + r + 1) * cap, 0:1]
             line = jnp.sum(hot * part_dots, axis=0, keepdims=True)
             route_out[origin] = jnp.broadcast_to(line, (8, count))
     for off in range(1, groups):
@@ -471,64 +599,98 @@
              route_recv.at[off - 1], {"expert": other})
     route_in[me] = route_out[me]
 
-    own = weight_slice(0)
+    values = weight_slice(dp)
+    for h in range(2):
+        for i, v in enumerate(pieces(*values, h)):
+            own[i, h] = v
+
+    give_back(1, last, False)
     for i in range(3):
-        grad_own[i] = own[i]
-
-    for t, ref in enumerate((out_ref, tgrad_ref)):
-        copy(partner.at[t, 0], partner.at[t, 0], pc_send.at[t, 0], pc_recv.at[t, 0],
-             {"expert": mate}).wait_recv()
-        value = expand(0, t, 3, 4)
-        wait_rows(has_up, chip + 1 == stages - 1, ret_in.at[t, chip], ret_recv.at[t, chip])
-        wait_rows(has_down, chip - 1 == 0, ret_down.at[t], retd_recv.at[t])
-        value += tn(up_hot.astype(BF16), ret_in[t, chip]) + tn(down_hot.astype(BF16), ret_down[t])
+        for k, where in ((0, to_y), (1, to_x)):
+            landed(grx.at[i, k], gr_recv.at[i, k])
+            gs2[i, k] = (keep[i, k] + grx[i, k].astype(F32)).astype(BF16)
+            send(None, gs2.at[i, k], grx.at[i, 4 + k], gr_send.at[i, 4 + k], gr_recv.at[i, 4 + k],
+                 where)
+    for q in near:
+        give_back(1, q, False)
+
+    stores = []
+
+    def store(src, dst):
+        cp = pltpu.make_async_copy(src, dst, store_sem.at[len(stores)])
+        cp.start()
+        stores.append(cp)
+
+    for t, (ref, hbm) in enumerate(((tok, out_hbm), (grad, tgrad_hbm))):
+        landed(yy.at[t, 0, pl.ds(cap, cap)], pc_recv.at[t, 0])
+        value = expand(t, 0, None, 3, 4)
+        for c in range(2):
+            wait_rows(has_up, chip + 1 == stages - 1, c, ret_in.at[t, chip], ret_recv.at[t, chip, c])
+            wait_rows(has_down, chip - 1 == 0, c, ret_down.at[t], retd_recv.at[t, c])
+        value += tn(up_hot, ret_in[t, chip]) + tn(down_hot, ret_down[t])
         ref[...] = value.astype(BF16)
+        store(ref, hbm)
 
     for off in range(1, groups):
         copy(route_out.at[0], route_in.at[0], route_send.at[off - 1], route_recv.at[off - 1],
-             {"expert": mate}).wait_recv()
+             to_mate).wait_recv()
     route_ref[...] = route_in[...]
-    for i, ref in enumerate((gg_ref, ug_ref, dg_ref)):
-        value = grad_own[i]
-        for off in range(1, ndp):
-            copy(grad_recv.at[i, off - 1], grad_recv.at[i, off - 1], gr_send.at[i, off - 1],
-                 gr_recv.at[i, off - 1], {"expert": mate}).wait_recv()
-            value += grad_recv[i, off - 1].astype(F32)
-        ref[...] = value.astype(BF16)
+    for i, hbm in enumerate((gg_hbm, ug_hbm, dg_hbm)):
+        for h in range(2):
+            value = own[i, h]
+            for k in (2 + h, 4 + h):
+                landed(grx.at[i, k], gr_recv.at[i, k])
+                value += grx[i, k].astype(F32)
+            gout[i, halves[h]] = value.astype(BF16)
+        store(gout.at[i], hbm)
     for cond, args in pending:
         if cond is None:
             copy(*args).wait_send()
         else:
             pl.when(cond)(lambda args=args: copy(*args).wait_send())
+    for cp in stores:
+        cp.wait()
 
 
 def kernel_scratch(groups, ndp, cap, count, width, part, ff):
     stages = groups // CORES
     rows = groups * cap
+    hp = part // 2
     shapes = [
+        ((count, width), BF16),
+        ((count, width), BF16),
         ((2, 2, stages, count, width), BF16),
         ((2, count, width), BF16),
         ((groups, 8, count), F32),
         ((rows, width), BF16),
         ((rows, width), BF16),
-        ((rows, width), BF16),
         ((rows, 128), F32),
-        ((3, ndp, part, ff), BF16),
-        ((2, rows, width), BF16),
+        ((ndp, part, 2 * ff), BF16),
+        ((ndp, part, ff), BF16),
+        ((2, stages, 2 * cap, width), BF16),
         ((2, stages, cap, width), BF16),
         ((2, stages, count, width), BF16),
         ((2, count, width), BF16),
         ((2, stages, count, width), BF16),
-        ((3, ndp - 1, part, ff), BF16),
-        ((3, part, ff), F32),
-        ((3, ndp - 1, part, ff), BF16),
+        ((rows, ff), F32),
+        ((rows, ff), F32),
+        ((rows, ff), BF16),
+        ((rows, ff), BF16),
+        ((rows, 2 * ff), BF16),
+        ((rows, 128), F32),
+        ((3, 4, hp, ff), BF16),
+        ((3, 2, hp, ff), BF16),
+        ((3, 6, hp, ff), BF16),
+        ((3, 2, hp, ff), F32),
+        ((3, 2, hp, ff), F32),
+        ((3, part, ff), BF16),
         ((groups, 8, count), F32),
         ((groups, 8, count), F32),
     ]
     sems = [
-        (2, stages, 3), (2, 2, stages), (groups - 1,), (groups - 1,), (3, ndp - 1), (3, ndp - 1),
-        (2, stages), (2, stages), (2, stages), (2, stages), (2,), (groups - 1,), (groups - 1,),
-        (3, ndp - 1), (3, ndp - 1),
+        (2, stages, 3, 2), (2, 2, stages, 2), (groups - 1,), (groups - 1,), (3, 6), (3, 6),
+        (2, stages), (2, stages), (2, stages, 2), (2, stages, 2), (2, 2), (groups - 1,),
+        (groups - 1,), (3, 6), (3, 6), (5,), (5,),
     ]
     return shapes, sems
 
@@ -557,6 +719,7 @@
     meta, order = route_tables(expert_ids, route_weights, groups)
     shapes, sems = kernel_scratch(groups, ndp, cap, count, width, part, ff)
     vmem = pl.BlockSpec(memory_space=pltpu.VMEM)
+    hbm = pl.BlockSpec(memory_space=pl.ANY)
     layer_out, token_grad, route, gate_g, up_g, down_g = pl.pallas_call(
         functools.partial(moe_kernel, groups, ndp, cap, edge),
         out_shape=(
@@ -567,8 +730,8 @@
             jax.ShapeDtypeStruct((part, ff), BF16),
             jax.ShapeDtypeStruct((part, ff), BF16),
         ),
-        in_specs=[vmem] * 7,
-        out_specs=(vmem,) * 6,
+        in_specs=[hbm, hbm, vmem, vmem, hbm, hbm, hbm],
+        out_specs=(hbm, hbm, vmem, hbm, hbm, hbm),
         scratch_shapes=[pltpu.VMEM(s, d) for s, d in shapes]
         + [pltpu.SemaphoreType.DMA(s) for s in sems],
         compiler_params=pltpu.CompilerParams(
@@ -585,10 +748,11 @@
     tokens, expert_ids, _, w_gate = args[:4]
     count, width = tokens.shape
     local, part, ff = w_gate.shape
-    if local == 1 and groups % CORES == 0 and groups > CORES and ndp > 1:
-        cap = pad16(slot_capacity(count, expert_ids.shape[1], groups))
-        shapes, _ = kernel_scratch(groups, ndp, cap, count, width, part, ff)
-        if scratch_bytes(shapes) < VMEM_MAX * 3 // 4:
+    if local == 1 and groups == 4 * CORES and ndp == 4:
+        slots = slot_capacity(count, expert_ids.shape[1], groups)
+        shapes, _ = kernel_scratch(groups, ndp, pad16(slots), count, width, part, ff)
+        tiled = count % 32 == 0 and part % 128 == 0 and ff % 128 == 0 and 4 * slots > count
+        if tiled and scratch_bytes(shapes) < VMEM_MAX * 9 // 10:
             return line_body(groups, ndp, *args)
     return body(*args)
 

time: 156 us -> 135 us (0.87)
  Pallas kernels: 143 us -> 121 us
    pallas_call x1, Pallas kernels: 143 us -> 121 us  [line_body(): pl.pallas_call(functools.partial(moe_kernel, groups, ndp, cap, edge), out...]
where the time goes in v1:
time: 135 us; the launch traced here: 134 us
  Pallas kernels  121 us (90%)
  local copies, waits for them, and re-layouts  9.15 us (7%)
  other arithmetic  2.32 us (2%)
    pallas_call x1, Pallas kernels, line_body(): pl.pallas_call(functools.partial(moe_kernel, groups, ndp, cap, edge), out...  121 us
    unnamed x17, local copies, waits for them, and re-layouts  7.5 us

profile of v1, /device:TPU:0, one launch (start us, length us, event | category | flops | bytes accessed | tf_op | source)
XLA Modules:
  0.0 133.6 jit_solution(7662461601071135806)
XLA Ops:
  0.7 0.1 pad.2.clone
  0.7 0.1 pad.3.clone
  0.8 0.0 copy-start.5
  0.8 0.7 copy-done.5
  1.5 0.0 copy-start.4
  1.5 0.7 copy-done.4
  2.2 0.1 convert_reduce_fusion
  2.3 0.1 convert_reduce_fusion.1
  2.4 0.7 maximum_maximum_fusion.order_ref
  3.1 0.1 broadcast_select_fusion
  3.2 0.2 multiply_reduce_fusion
  3.4 0.1 compare_select_fusion.3
  3.5 0.4 fusion.1
  4.0 0.7 stack.27.meta_ref
  4.7 121.4 %shard_map.118 = (bf16[128,2048]{1,0:T(8,128)(2,1)}, bf16[128,2048]{1,0:T(8,128)(2,1)}, f32[8,8,128]{2,1,0:T(8,128)}, bf16[512,384]{1,0:T(8,128)(2,1)}, bf16[512...) custom-call(bf16[128,2048]{1,0:T(8,128)(2,1)} %tok_hbm.1, bf16[128,2048]{1,0:T(8,128)(2,1)} %grad_hbm.1, ...), custom_call_target="tpu_custom_call" | custom-call | tf_op jit(solution)/shard_map/pallas_call | solution.py:723
  126.1 0.8 slice.19
  126.8 0.6 select_reduce_fusion
  127.4 0.0 copy-start
  127.4 1.9 %copy.19 = bf16[128,2048]{1,0:T(8,128)(2,1)} copy(bf16[128,2048]{1,0:T(8,128)(2,1)} %get-tuple-element.36) | data formatting | bytes 1048576
  129.4 0.0 copy-done
  129.4 0.0 copy-start.3
  129.4 0.8 copy.20
  130.2 0.4 copy-done.3
  130.6 0.0 copy-start.2
  130.6 0.7 copy.21
  131.3 0.4 copy-done.2
  131.7 0.0 copy-start.1
  131.7 0.7 copy.22
  132.4 0.4 copy-done.1
  132.8 0.7 copy.23
  (17 shorter events, 0.2 us)
Async XLA Ops:
  0.8 0.7 copy-start.5
  1.5 0.7 copy-start.4
  127.4 1.9 %copy-start = (bf16[128,2048]{1,0:T(8,128)(2,1)S(1)}, bf16[128,2048]{1,0:T(8,128)(2,1)}, u32[]{:S(2)}) copy-start(bf16[128,2048]{1,0:T(8,128)(2,1)} %get-tuple-element.37) | copy-start | bytes 1572868
  129.4 1.2 copy-start.3
  130.6 1.1 copy-start.2
  131.7 1.1 copy-start.1

commit v2 on v1

--- a/solution.py
+++ b/solution.py
@@ -10,7 +10,7 @@
 BF16 = jnp.bfloat16
 F32 = jnp.float32
 CORES = 2
-VMEM_MAX = 60 * 1024 * 1024
+VMEM_MAX = 56 * 1024 * 1024
 
 
 def slot_table(expert_ids, experts, capacity):
@@ -152,44 +152,50 @@
     return (n + 15) // 16 * 16
 
 
-def prefix_count(member):
-    t = member.shape[1]
-    before = lax.broadcasted_iota(jnp.int32, (t, t), 0) < lax.broadcasted_iota(jnp.int32, (t, t), 1)
-    return jnp.sum(member[:, :, None] * before.astype(F32)[None], axis=1)
-
-
-def route_tables(expert_ids, route_weights, groups):
-    count, top = expert_ids.shape
+def route_tables(ids, weights, groups, chip):
+    top, count = ids.shape
     stages = groups // CORES
-    chip = lax.axis_index("expert") // CORES
-    lanes = lax.broadcasted_iota(jnp.int32, (count,), 0)
+    lanes = lax.broadcasted_iota(jnp.int32, (1, count), 1).astype(F32)
     experts = lax.broadcasted_iota(jnp.int32, (groups, count), 0)
-    member = jnp.zeros((groups, count), F32)
-    weight = jnp.zeros((groups, count), F32)
-    for k in range(top):
-        hit = (expert_ids[:, k][None, :] == experts).astype(F32)
-        member = member + hit
-        weight = weight + hit * route_weights[:, k][None, :]
-    slot = jnp.where(member > 0, prefix_count(member), -1.0)
-
-    def position(first):
-        key = jnp.where(first, lanes, lanes + count)
-        return jnp.sum((key[:, None] < key[None, :]).astype(F32), axis=0)
-
-    pos_up = position(jnp.any(expert_ids // CORES == stages - 1, axis=1))
-    pos_down = position(jnp.any(expert_ids // CORES == 0, axis=1))
-    dest = lax.broadcasted_iota(jnp.int32, (groups, 1), 0) // CORES
-    pos = jnp.where(dest >= chip, pos_up[None, :], pos_down[None, :])
-    pick = (pos[:, None, :] == lanes.astype(F32)[None, :, None]).astype(F32)
-    slot_rows = jnp.sum(pick * slot[:, None, :], axis=2)
-    weight_rows = jnp.sum(pick * weight[:, None, :], axis=2)
-    swap = lambda a: a.reshape(stages, CORES, count)[:, ::-1].reshape(groups, count)
-    zero = jnp.zeros_like(slot)
-    meta = jnp.stack(
-        [slot_rows, weight_rows, swap(slot_rows), slot, swap(slot), zero, zero, zero], axis=1
-    )
-    order = jnp.stack([pos_up, pos_down] + [jnp.zeros_like(pos_up)] * 6, axis=0)
-    return meta, order
+    hits = [(ids[k:k + 1, :] == experts).astype(F32) for k in range(top)]
+    member = sum(hits)
+    weight = sum(hit * weights[k:k + 1, :] for k, hit in enumerate(hits))
+    first_up = sum(member[groups - CORES + i:groups - CORES + i + 1] for i in range(CORES))
+    first_down = sum(member[i:i + 1] for i in range(CORES))
+    first = [(f > 0).astype(F32) for f in (first_up, first_down)]
+    before = (
+        lax.broadcasted_iota(jnp.int32, (count, count), 0) < lax.broadcasted_iota(jnp.int32, (count, count), 1)
+    ).astype(BF16)
+    counts = jnp.dot(jnp.concatenate([member] + first + [jnp.zeros((groups - 2, count), F32)], axis=0).astype(BF16),
+                     before, preferred_element_type=F32)
+    slot = jnp.where(member > 0, counts[:groups], -1.0)
+
+    def position(i):
+        ahead = counts[groups + i:groups + i + 1]
+        number = jnp.sum(first[i], axis=1, keepdims=True)
+        return jnp.where(first[i] > 0, ahead, number + lanes - ahead)
+
+    hots = [one_hot(position(i), count) for i in range(2)]
+    dest = lax.broadcasted_iota(jnp.int32, (groups, count), 0) // CORES
+
+    def in_order(values, precision):
+        up, down = [
+            lax.dot_general(values, hot.astype(values.dtype), (((1,), (1,)), ((), ())),
+                            precision=precision, preferred_element_type=F32)
+            for hot in hots
+        ]
+        return jnp.where(dest >= chip, up, down)
+
+    slot_rows = in_order(slot.astype(BF16), None)
+    weight_rows = in_order(weight, lax.Precision.HIGHEST)
+    tiles = []
+    for e in range(groups):
+        other = e // CORES * CORES + (CORES - 1 - e % CORES)
+        row = lambda a, i: a[i:i + 1]
+        tiles.append(jnp.concatenate(
+            [row(slot_rows, e), row(weight_rows, e), row(slot_rows, other), row(slot, e), row(slot, other),
+             jnp.zeros((3, count), F32)], axis=0))
+    return tiles, hots[0].astype(BF16), hots[1].astype(BF16), hits
 
 
 def one_hot(row, height):
@@ -212,16 +218,16 @@
 
 def moe_kernel(
     groups, ndp, cap, edge,
-    tok_hbm, grad_hbm, meta_ref, order_ref, wg_hbm, wu_hbm, wd_hbm,
-    out_hbm, tgrad_hbm, route_ref, gg_hbm, ug_hbm, dg_hbm,
-    tok, grad, blocks, own_down, metas, xr, gr, wr, wgu, wd, yy, ym, ret_in, ret_down, ret_out,
-    fa, fb, hid, hs, both, dots, gs, gs2, grx, keep, own, gout, route_out, route_in,
+    tok_hbm, grad_hbm, ids_ref, weight_ref, wg_hbm, wu_hbm, wd_hbm,
+    out_ref, tgrad_ref, route_ref, gg_ref, ug_ref, dg_ref,
+    tok, grad, meta_own, blocks, own_down, metas, xr, gr, wr, wgu, wd, yy, ym, ret_in, ret_down, ret_out,
+    fa, fb, hid, hs, both, dots, gs, gs2, grx, keep, own, route_out, route_in,
     in_send, in_recv, meta_send, meta_recv, w_send, w_recv, pc_send, pc_recv,
-    ret_send, ret_recv, retd_recv, route_send, route_recv, gr_send, gr_recv, load_sem, store_sem,
+    ret_send, ret_recv, retd_recv, route_send, route_recv, gr_send, gr_recv, load_sem,
 ):
     stages = groups // CORES
     count, width = tok.shape
-    part, ff = gout.shape[1:]
+    part, ff = gg_ref.shape
     half, hp = count // 2, part // 2
     me = lax.axis_index("expert")
     dp = lax.axis_index("dp")
@@ -299,36 +305,6 @@
     for load in loads:
         load.start()
 
-    if edge < count:
-        rest = pl.ds(edge, count - edge)
-        empty = jnp.zeros((count - edge, width), BF16)
-        for t in range(2):
-            for s in range(stages):
-                blocks[0, t, s, rest] = empty
-                blocks[1, t, s, rest] = empty
-                ret_in[t, s, rest] = empty
-            ret_down[t, rest] = empty
-    for t in range(2):
-        @pl.when(chip == stages - 1)
-        def _():
-            ret_in[t, chip] = jnp.zeros((count, width), BF16)
-
-        @pl.when(chip == 0)
-        def _():
-            ret_down[t] = jnp.zeros((count, width), BF16)
-
-    up_hot = one_hot(order_ref[0:1, :], count).astype(BF16)
-    down_hot = one_hot(order_ref[1:2, :], count).astype(BF16)
-    metas[me] = meta_ref[me]
-
-    def arrange(t):
-        value = (tok, grad)[t][...]
-        blocks[0, t, chip] = nn(up_hot, value).astype(BF16)
-        own_down[t] = nn(down_hot, value).astype(BF16)
-
-    loads[0].wait()
-    arrange(0)
-
     barrier = pltpu.get_barrier_semaphore()
     for off in range(1, groups):
         pl.semaphore_signal(barrier, inc=1, device_id={"expert": (me + off) % groups},
@@ -336,15 +312,27 @@
     for off in range(1, ndp):
         pl.semaphore_signal(barrier, inc=1, device_id={"dp": (dp + off) % ndp},
                             device_id_type=pl.DeviceIdType.MESH)
+
+    tiles, up_hot, down_hot, hits = route_tables(ids_ref[...], weight_ref[...], groups, chip)
+    for e in range(groups):
+        meta_own[e] = tiles[e]
+
+    def arrange(t):
+        value = (tok, grad)[t][...]
+        blocks[0, t, chip] = nn(up_hot, value).astype(BF16)
+        own_down[t] = nn(down_hot, value).astype(BF16)
+
+    loads[0].wait()
+    arrange(0)
     pl.semaphore_wait(barrier, groups + ndp - 2)
 
-    def depart_up(t, cond):
-        for c in range(2):
+    def depart_up(t, cond, chunks=(0, 1)):
+        for c in chunks:
             send_rows(cond, chip + 1 == stages - 1, c, blocks.at[0, t, chip], blocks.at[0, t, chip],
                       in_send.at[t, 0, 0, c], in_recv.at[0, t, chip, c], up_dev)
 
-    def depart_down(t, cond):
-        for c in range(2):
+    def depart_down(t, cond, chunks=(0, 1)):
+        for c in chunks:
             send_rows(cond, chip - 1 == 0, c, own_down.at[t], blocks.at[0, t, chip],
                       in_send.at[t, 0, 1, c], in_recv.at[0, t, chip, c], down_dev)
 
@@ -374,32 +362,64 @@
     depart_mate(0)
     for off in range(1, groups):
         other = (me + off) % groups
-        send(None, meta_ref.at[other], metas.at[me], meta_send.at[off - 1], meta_recv.at[off - 1],
+        send(None, meta_own.at[other], metas.at[me], meta_send.at[off - 1], meta_recv.at[off - 1],
              {"expert": other})
     for i in range(2):
         loads[1 + i].wait()
         weight_direct(i)
+    metas[me] = meta_own[me]
+    if edge < count:
+        rest = pl.ds(edge, count - edge)
+        empty = jnp.zeros((count - edge, width), BF16)
+        for s in range(stages):
+            ends_at = jnp.where(s > chip, chip - 1, chip + 1)
+            from_edge = (s != chip) & inside & ((ends_at == 0) | (ends_at == stages - 1))
+
+            @pl.when(at_edge & (s != chip))
+            def _():
+                for t in range(2):
+                    blocks[0, t, s, rest] = empty
+                    blocks[1, t, s, rest] = empty
+
+            @pl.when(from_edge | ((s == chip) & (chip + 1 == stages - 1)))
+            def _():
+                for t in range(2):
+                    ret_in[t, s, rest] = empty
+
+        @pl.when(chip - 1 == 0)
+        def _():
+            for t in range(2):
+                ret_down[t, rest] = empty
+    for t in range(2):
+        @pl.when(chip == stages - 1)
+        def _():
+            ret_in[t, chip] = jnp.zeros((count, width), BF16)
+
+        @pl.when(chip == 0)
+        def _():
+            ret_down[t] = jnp.zeros((count, width), BF16)
+
     loads[3].wait()
     arrange(1)
     depart_up(1, has_up & at_edge)
     depart_down(1, has_down & at_edge)
     depart_mate(1)
     for off in range(1, groups):
-        copy(meta_ref.at[0], metas.at[0], meta_send.at[off - 1], meta_recv.at[off - 1],
+        copy(meta_own.at[0], metas.at[0], meta_send.at[off - 1], meta_recv.at[off - 1],
              to_mate).wait_recv()
 
     table = [visit_order(z, stages) for z in range(stages)]
     source = [choose(chip, [table[z][q] for z in range(stages)]) for q in range(stages)]
 
-    def arrive(t, q, c):
+    def arrive(t, q, c, role=yes):
         s = source[q]
         nxt = jnp.where(s < chip, chip + 1, chip - 1)
         more = (nxt >= 0) & (nxt < stages)
-        wait_rows(yes, at_edge, c, blocks.at[0, t, s], in_recv.at[0, t, s, c])
-        send_rows(more, (nxt == 0) | (nxt == stages - 1), c, blocks.at[0, t, s],
+        wait_rows(role, at_edge, c, blocks.at[0, t, s], in_recv.at[0, t, s, c])
+        send_rows(more & role, (nxt == 0) | (nxt == stages - 1), c, blocks.at[0, t, s],
                   blocks.at[0, t, s], in_send.at[t, q, 0, c], in_recv.at[0, t, s, c],
                   {"expert": nxt * CORES + core})
-        send_rows(None, at_edge, c, blocks.at[0, t, s], blocks.at[1, t, s],
+        send_rows(role, at_edge, c, blocks.at[0, t, s], blocks.at[1, t, s],
                   in_send.at[t, q, 2, c], in_recv.at[1, t, s, c], to_mate)
 
     def compact(t, q):
@@ -431,12 +451,15 @@
         arrive(0, q, 1)
     for q in near:
         compact(0, q)
+    high = jnp.logical_not(low)
+    depart_up(1, inside & high, (1,))
+    depart_down(1, inside & low, (1,))
     arrive(0, last, 0)
     depart_up(1, inside & low)
-    depart_down(1, inside & jnp.logical_not(low))
+    depart_down(1, inside & high)
     arrive(0, last, 1)
-    depart_up(1, inside & jnp.logical_not(low))
-    depart_down(1, inside & low)
+    depart_up(1, inside & high, (0,))
+    depart_down(1, inside & low, (0,))
     compact(0, last)
     for i in range(2):
         weight_rest(i)
@@ -461,13 +484,13 @@
     fa[...] = scale * (up * sig * (1.0 + gate * (1.0 - sig)))
     fb[...] = scale * gated
 
-    for q in near:
-        arrive(1, q, 0)
+    arrive(1, 1, 0)
+    for q in near[1:]:
+        arrive(1, q, 0, inside)
     weight_relay(2)
-    for q in near:
-        arrive(1, q, 1)
-    for q in range(last):
-        compact(1, q)
+    arrive(1, 1, 1)
+    for q in near[1:]:
+        arrive(1, q, 1, inside)
 
     def place(t, cols, value, qs):
         for n, q in enumerate(qs):
@@ -523,7 +546,7 @@
             send(here & jnp.logical_not(arrives), ret_out.at[t, q, rows], ret_in.at[t, s, rows],
                  ret_send.at[t, q, c], ret_recv.at[t, s, c], where)
 
-    def backward(qs):
+    def backward_hidden(qs):
         rows = pl.ds(qs[0] * 2 * cap, len(qs) * 2 * cap)
         hg = nn(gr[rows, cut(0)], wd[0])
         for j in range(1, ndp):
@@ -532,6 +555,9 @@
         both[rows, ff:] = (hg * fb[rows, :]).astype(BF16)
         line = jnp.sum(hg * hid[rows, :].astype(F32), axis=1, keepdims=True)
         dots[rows, :] = jnp.broadcast_to(line, (line.shape[0], 128))
+
+    def backward_rows(qs):
+        rows = pl.ds(qs[0] * 2 * cap, len(qs) * 2 * cap)
         for j in range(ndp):
             place(1, cut(j), nt(both[rows, :], wgu[j]).astype(BF16), qs)
         pair(1, qs)
@@ -540,11 +566,20 @@
     for q in reversed(near):
         if q > 1:
             give_back(0, q, True)
-    arrive(1, last, 0)
-    backward(range(last))
-    arrive(1, last, 1)
+    arrive(1, last, 0, inside)
+    compact(1, 0)
+    compact(1, 1)
+    for q in near[1:]:
+        for c in range(2):
+            arrive(1, q, c, at_edge)
+        compact(1, q)
+    backward_hidden(range(last))
+    arrive(1, last, 1, inside)
+    backward_rows(range(last))
+    for c in range(2):
+        arrive(1, last, c, at_edge)
     compact(1, last)
-    backward(range(last, stages))
+    backward_hidden(range(last, stages))
 
     def weight_slice(j):
         cols = cut_at(j)
@@ -570,11 +605,12 @@
     values = weight_slice(dg)
     give_grad(0, 0, values, to_x)
     give_grad(1, 1, values, to_y)
+    backward_rows(range(last, stages))
     give_back(0, last, False)
-    give_back(1, last, True)
     values = weight_slice(xn)
     give_grad(2, 0, values, to_x)
     keep_grad(1, 1, values)
+    give_back(1, last, True)
     values = weight_slice(yn)
     give_grad(3, 1, values, to_y)
     keep_grad(0, 0, values)
@@ -614,14 +650,7 @@
     for q in near:
         give_back(1, q, False)
 
-    stores = []
-
-    def store(src, dst):
-        cp = pltpu.make_async_copy(src, dst, store_sem.at[len(stores)])
-        cp.start()
-        stores.append(cp)
-
-    for t, (ref, hbm) in enumerate(((tok, out_hbm), (grad, tgrad_hbm))):
+    for t, ref in enumerate((out_ref, tgrad_ref)):
         landed(yy.at[t, 0, pl.ds(cap, cap)], pc_recv.at[t, 0])
         value = expand(t, 0, None, 3, 4)
         for c in range(2):
@@ -629,27 +658,46 @@
             wait_rows(has_down, chip - 1 == 0, c, ret_down.at[t], retd_recv.at[t, c])
         value += tn(up_hot, ret_in[t, chip]) + tn(down_hot, ret_down[t])
         ref[...] = value.astype(BF16)
-        store(ref, hbm)
 
     for off in range(1, groups):
         copy(route_out.at[0], route_in.at[0], route_send.at[off - 1], route_recv.at[off - 1],
              to_mate).wait_recv()
-    route_ref[...] = route_in[...]
-    for i, hbm in enumerate((gg_hbm, ug_hbm, dg_hbm)):
+    for k, hit in enumerate(hits):
+        line = sum(hit[e:e + 1] * route_in[e, 0:1] for e in range(groups))
+        route_ref[k:k + 1, :] = line
+    for i, ref in enumerate((gg_ref, ug_ref, dg_ref)):
         for h in range(2):
             value = own[i, h]
             for k in (2 + h, 4 + h):
                 landed(grx.at[i, k], gr_recv.at[i, k])
                 value += grx[i, k].astype(F32)
-            gout[i, halves[h]] = value.astype(BF16)
-        store(gout.at[i], hbm)
+            ref[halves[h]] = value.astype(BF16)
     for cond, args in pending:
         if cond is None:
             copy(*args).wait_send()
         else:
             pl.when(cond)(lambda args=args: copy(*args).wait_send())
-    for cp in stores:
+
+
+def flush_kernel(*refs):
+    number = (len(refs) - 1) // 2
+    copies = [
+        pltpu.make_async_copy(refs[n], refs[number + n], refs[-1].at[n]) for n in range(number)
+    ]
+    for cp in copies:
+        cp.start()
+    for cp in copies:
         cp.wait()
+
+
+def flush(*arrays):
+    return pl.pallas_call(
+        flush_kernel,
+        out_shape=tuple(jax.ShapeDtypeStruct(a.shape, a.dtype) for a in arrays),
+        in_specs=[pl.BlockSpec(memory_space=pltpu.VMEM)] * len(arrays),
+        out_specs=(pl.BlockSpec(memory_space=pltpu.HBM),) * len(arrays),
+        scratch_shapes=[pltpu.SemaphoreType.DMA((len(arrays),))],
+    )(*(pltpu.with_memory_space_constraint(a, pltpu.VMEM) for a in arrays))
 
 
 def kernel_scratch(groups, ndp, cap, count, width, part, ff):
@@ -659,6 +707,7 @@
     shapes = [
         ((count, width), BF16),
         ((count, width), BF16),
+        ((groups, 8, count), F32),
         ((2, 2, stages, count, width), BF16),
         ((2, count, width), BF16),
         ((groups, 8, count), F32),
@@ -683,14 +732,13 @@
         ((3, 6, hp, ff), BF16),
         ((3, 2, hp, ff), F32),
         ((3, 2, hp, ff), F32),
-        ((3, part, ff), BF16),
         ((groups, 8, count), F32),
         ((groups, 8, count), F32),
     ]
     sems = [
         (2, stages, 3, 2), (2, 2, stages, 2), (groups - 1,), (groups - 1,), (3, 6), (3, 6),
         (2, stages), (2, stages), (2, stages, 2), (2, stages, 2), (2, 2), (groups - 1,),
-        (groups - 1,), (3, 6), (3, 6), (5,), (5,),
+        (groups - 1,), (3, 6), (3, 6), (5,),
     ]
     return shapes, sems
 
@@ -716,32 +764,29 @@
     slots = slot_capacity(count, top, groups)
     cap = pad16(slots)
     edge = min(count, pad16(CORES * slots))
-    meta, order = route_tables(expert_ids, route_weights, groups)
     shapes, sems = kernel_scratch(groups, ndp, cap, count, width, part, ff)
     vmem = pl.BlockSpec(memory_space=pltpu.VMEM)
-    hbm = pl.BlockSpec(memory_space=pl.ANY)
-    layer_out, token_grad, route, gate_g, up_g, down_g = pl.pallas_call(
+    hbm = pl.BlockSpec(memory_space=pltpu.HBM)
+    outs = pl.pallas_call(
         functools.partial(moe_kernel, groups, ndp, cap, edge),
         out_shape=(
-            jax.ShapeDtypeStruct((count, width), BF16),
-            jax.ShapeDtypeStruct((count, width), BF16),
-            jax.ShapeDtypeStruct((groups, 8, count), F32),
-            jax.ShapeDtypeStruct((part, ff), BF16),
-            jax.ShapeDtypeStruct((part, ff), BF16),
-            jax.ShapeDtypeStruct((part, ff), BF16),
+            pltpu.VMEM((count, width), BF16),
+            pltpu.VMEM((count, width), BF16),
+            pltpu.VMEM((top, count), F32),
+            pltpu.VMEM((part, ff), BF16),
+            pltpu.VMEM((part, ff), BF16),
+            pltpu.VMEM((part, ff), BF16),
         ),
         in_specs=[hbm, hbm, vmem, vmem, hbm, hbm, hbm],
-        out_specs=(hbm, hbm, vmem, hbm, hbm, hbm),
+        out_specs=(vmem,) * 6,
         scratch_shapes=[pltpu.VMEM(s, d) for s, d in shapes]
         + [pltpu.SemaphoreType.DMA(s) for s in sems],
         compiler_params=pltpu.CompilerParams(
             collective_id=0, has_side_effects=True, vmem_limit_bytes=VMEM_MAX
         ),
-    )(tokens, grad_out, meta, order, w_gate[0], w_up[0], w_down[0])
-    experts = lax.broadcasted_iota(jnp.int32, (groups, count, top), 0)
-    mine = (expert_ids[None] == experts).astype(F32)
-    route_grad = jnp.sum(mine * route[:, 0, :, None], axis=0)
-    return layer_out, token_grad, route_grad, gate_g[None], up_g[None], down_g[None]
+    )(tokens, grad_out, expert_ids.T, route_weights.T, w_gate[0], w_up[0], w_down[0])
+    layer_out, token_grad, route, gate_g, up_g, down_g = flush(*outs)
+    return layer_out, token_grad, route.T, gate_g[None], up_g[None], down_g[None]
 
 
 def pick_body(groups, ndp, *args):

time: 135 us -> 115 us (0.85); the launches traced: 134 us -> 115 us
  local copies, waits for them, and re-layouts: 9.15 us -> 0 us
  Pallas kernels: 121 us -> 114 us
  other arithmetic: 2.32 us -> 0 us
    pallas_call x1, Pallas kernels: 121 us -> 113 us  [line_body(): pl.pallas_call(functools.partial(moe_kernel, groups, ndp, cap, edge), out...]
    unnamed x17 -> x0, local copies, waits for them, and re-layouts: 7.5 us -> none
    reduce_sum x5 -> x0, other arithmetic: 1.42 us -> none  [the longest x1 0.58 us: line_body(): route_grad = jnp.sum(mine * route[:, 0, :, None], axis=0)]
    pallas_call x0 -> x1, Pallas kernels: none -> 1.41 us  [flush(): pl.pallas_call(flush_kernel, out_shape=tuple((jax.ShapeDtypeStruct(a.shap...]
where the time goes in v2:
time: 115 us
  Pallas kernels  114 us (99%)
    pallas_call x1, Pallas kernels, line_body(): pl.pallas_call(functools.partial(moe_kernel, groups, ndp, cap, edge), out...  113 us

profile of v2, /device:TPU:0, one launch (start us, length us, event | category | flops | bytes accessed | tf_op | source)
XLA Modules:
  0.0 115.2 jit_solution(14334952859507000799)
XLA Ops:
  0.6 113.0 %shard_map.118 = (bf16[128,2048]{1,0:T(8,128)(2,1)S(1)}, bf16[128,2048]{1,0:T(8,128)(2,1)S(1)}, f32[2,128]{1,0:T(2,128)S(1)}, bf16[512,384]{1,0:T(8,128)(2,1)S(1...) custom-call(bf16[128,2048]{1,0:T(8,128)(2,1)} %tok_hbm.1, bf16[128,2048]{1,0:T(8,128)(2,1)} %grad_hbm.1, ...), custom_call_target="tpu_custom_call" | custom-call | tf_op jit(solution)/shard_map/pallas_call | solution.py:770
  113.6 1.4 %shard_map.119 = (bf16[128,2048]{1,0:T(8,128)(2,1)}, bf16[128,2048]{1,0:T(8,128)(2,1)}, f32[2,128]{1,0:T(2,128)}, bf16[512,384]{1,0:T(8,128)(2,1)}, bf16[512,384]{1,0:T(8,128)(2,1)}, /*index=5*/bf16[512,384]{1,0:T(8,128)(2,1)}) custom-call(bf16[128,2048]{1,0:T(8,128)(2,1)S(1)} %get-tuple-element.18.refs_0_, bf16[128,2048]{1,0:T(8,128)(2,1)S(1)} %get-tuple-element.19.refs_1_, ...), custom_call_target="tpu_custom_call" | custom-call | tf_op jit(solution)/shard_map/pallas_call | solution.py:694

commit v3 on v2

--- a/solution.py
+++ b/solution.py
@@ -221,7 +221,7 @@
     tok_hbm, grad_hbm, ids_ref, weight_ref, wg_hbm, wu_hbm, wd_hbm,
     out_ref, tgrad_ref, route_ref, gg_ref, ug_ref, dg_ref,
     tok, grad, meta_own, blocks, own_down, metas, xr, gr, wr, wgu, wd, yy, ym, ret_in, ret_down, ret_out,
-    fa, fb, hid, hs, both, dots, gs, gs2, grx, keep, own, route_out, route_in,
+    fa, fb, hid, hs, both, dots, gs, gs2, grx, keep, own, ex, route_out, route_in,
     in_send, in_recv, meta_send, meta_recv, w_send, w_recv, pc_send, pc_recv,
     ret_send, ret_recv, retd_recv, route_send, route_recv, gr_send, gr_recv, load_sem,
 ):
@@ -353,8 +353,9 @@
             landed(ref, w_recv.at[i, n])
             send(None, ref, ref, w_send.at[i, 4 + n], w_recv.at[i, 4 + n], where)
 
-    def weight_rest(i):
-        for n, (h, j) in ((2, (1, xn)), (3, (0, yn)), (4, (0, dg)), (5, (1, dg))):
+    def weight_rest(i, ns=range(2, 6)):
+        for n in ns:
+            h, j = ((1, xn), (0, yn), (0, dg), (1, dg))[n - 2]
             landed(weight(i, j).at[halves[h]], w_recv.at[i, n])
 
     depart_up(0, has_up)
@@ -484,10 +485,10 @@
     fa[...] = scale * (up * sig * (1.0 + gate * (1.0 - sig)))
     fb[...] = scale * gated
 
+    weight_relay(2)
     arrive(1, 1, 0)
     for q in near[1:]:
         arrive(1, q, 0, inside)
-    weight_relay(2)
     arrive(1, 1, 1)
     for q in near[1:]:
         arrive(1, q, 1, inside)
@@ -505,18 +506,26 @@
     everyone = range(stages)
     for n, j in enumerate((dp, xn, yn, dg)):
         if n == 1:
-            weight_rest(2)
+            weight_rest(2, (2, 3))
+        if n == 3:
+            weight_rest(2, (4, 5))
         place(0, cut_at(j), nt(hs[...], wd[j]).astype(BF16), everyone)
     pair(0, everyone)
 
-    def expand(t, q, c, row_own, row_mate):
+    def expand(t, q, row_own, row_mate):
         tile = metas[source[q] * CORES + core]
         hot = jnp.concatenate(
             [one_hot(tile[row_own:row_own + 1, :], cap), one_hot(tile[row_mate:row_mate + 1, :], cap)],
             axis=0).astype(BF16)
-        if c is not None:
-            hot = hot[:, c * half:(c + 1) * half]
         return tn(hot, yy[t, q])
+
+    bounds = (0, half // 2, half, edge, count)
+    chunks = [pl.ds(lo, hi - lo) for lo, hi in zip(bounds, bounds[1:])]
+
+    def wait_chunk(cond, short, k, dst, sem):
+        if k == len(chunks) - 1:
+            cond = cond & jnp.logical_not(short)
+        pl.when(cond)(lambda: landed(dst.at[chunks[k]], sem))
 
     def give_back(t, q, ends):
         s = source[q]
@@ -526,25 +535,30 @@
         where = {"expert": nxt * CORES + core}
         here = at_edge if ends else inside
         arrives = rising & (nxt == s)
-        pl.when(here)(lambda: landed(yy.at[t, q, pl.ds(cap, cap)], pc_recv.at[t, q]))
-        for c in range(2):
-            lines = pl.ds(c * half, half)
+        short = (back == 0) | (back == stages - 1)
+
+        @pl.when(here)
+        def _():
+            landed(yy.at[t, q, pl.ds(cap, cap)], pc_recv.at[t, q])
+            ex[...] = expand(t, q, 0, 2)
+
+        for k, rows in enumerate(chunks):
+            if ends and k == len(chunks) - 1:
+                continue
             if not ends:
-                wait_rows(here, (back == 0) | (back == stages - 1), c, ret_in.at[t, s],
-                          ret_recv.at[t, s, c])
+                wait_chunk(here, short, k, ret_in.at[t, s], ret_recv.at[t, s, k])
 
             @pl.when(here)
             def _():
-                value = expand(t, q, c, 0, 2)
+                value = ex[rows]
                 if not ends:
-                    value = value + ret_in[t, s, lines].astype(F32)
-                ret_out[t, q, lines] = value.astype(BF16)
-
-            rows = rows_of(c, ends)
-            send(here & arrives, ret_out.at[t, q, rows], ret_down.at[t, rows], ret_send.at[t, q, c],
-                 retd_recv.at[t, c], where)
+                    value = value + ret_in[t, s, rows].astype(F32)
+                ret_out[t, q, rows] = value.astype(BF16)
+
+            send(here & arrives, ret_out.at[t, q, rows], ret_down.at[t, rows], ret_send.at[t, q, k],
+                 retd_recv.at[t, k], where)
             send(here & jnp.logical_not(arrives), ret_out.at[t, q, rows], ret_in.at[t, s, rows],
-                 ret_send.at[t, q, c], ret_recv.at[t, s, c], where)
+                 ret_send.at[t, q, k], ret_recv.at[t, s, k], where)
 
     def backward_hidden(qs):
         rows = pl.ds(qs[0] * 2 * cap, len(qs) * 2 * cap)
@@ -576,6 +590,7 @@
     backward_hidden(range(last))
     arrive(1, last, 1, inside)
     backward_rows(range(last))
+    give_back(0, last, False)
     for c in range(2):
         arrive(1, last, c, at_edge)
     compact(1, last)
@@ -606,7 +621,6 @@
     give_grad(0, 0, values, to_x)
     give_grad(1, 1, values, to_y)
     backward_rows(range(last, stages))
-    give_back(0, last, False)
     values = weight_slice(xn)
     give_grad(2, 0, values, to_x)
     keep_grad(1, 1, values)
@@ -650,28 +664,35 @@
     for q in near:
         give_back(1, q, False)
 
-    for t, ref in enumerate((out_ref, tgrad_ref)):
+    def finish(t, ref):
+        for k in range(len(chunks)):
+            wait_chunk(has_up, chip + 1 == stages - 1, k, ret_in.at[t, chip], ret_recv.at[t, chip, k])
+            wait_chunk(has_down, chip - 1 == 0, k, ret_down.at[t], retd_recv.at[t, k])
+        value = ex[...] + tn(up_hot, ret_in[t, chip]) + tn(down_hot, ret_down[t])
+        ref[...] = value.astype(BF16)
+
+    def stay(t):
         landed(yy.at[t, 0, pl.ds(cap, cap)], pc_recv.at[t, 0])
-        value = expand(t, 0, None, 3, 4)
-        for c in range(2):
-            wait_rows(has_up, chip + 1 == stages - 1, c, ret_in.at[t, chip], ret_recv.at[t, chip, c])
-            wait_rows(has_down, chip - 1 == 0, c, ret_down.at[t], retd_recv.at[t, c])
-        value += tn(up_hot, ret_in[t, chip]) + tn(down_hot, ret_down[t])
-        ref[...] = value.astype(BF16)
-
+        ex[...] = expand(t, 0, 3, 4)
+
+    stay(0)
+    finish(0, out_ref)
+    stay(1)
     for off in range(1, groups):
         copy(route_out.at[0], route_in.at[0], route_send.at[off - 1], route_recv.at[off - 1],
              to_mate).wait_recv()
     for k, hit in enumerate(hits):
         line = sum(hit[e:e + 1] * route_in[e, 0:1] for e in range(groups))
         route_ref[k:k + 1, :] = line
+    for i in range(3):
+        for h in range(2):
+            landed(grx.at[i, 2 + h], gr_recv.at[i, 2 + h])
+            own[i, h] = own[i, h] + grx[i, 2 + h].astype(F32)
+    finish(1, tgrad_ref)
     for i, ref in enumerate((gg_ref, ug_ref, dg_ref)):
         for h in range(2):
-            value = own[i, h]
-            for k in (2 + h, 4 + h):
-                landed(grx.at[i, k], gr_recv.at[i, k])
-                value += grx[i, k].astype(F32)
-            ref[halves[h]] = value.astype(BF16)
+            landed(grx.at[i, 4 + h], gr_recv.at[i, 4 + h])
+            ref[halves[h]] = (own[i, h] + grx[i, 4 + h].astype(F32)).astype(BF16)
     for cond, args in pending:
         if cond is None:
             copy(*args).wait_send()
@@ -732,12 +753,13 @@
         ((3, 6, hp, ff), BF16),
         ((3, 2, hp, ff), F32),
         ((3, 2, hp, ff), F32),
+        ((count, width), F32),
         ((groups, 8, count), F32),
         ((groups, 8, count), F32),
     ]
     sems = [
         (2, stages, 3, 2), (2, 2, stages, 2), (groups - 1,), (groups - 1,), (3, 6), (3, 6),
-        (2, stages), (2, stages), (2, stages, 2), (2, stages, 2), (2, 2), (groups - 1,),
+        (2, stages), (2, stages), (2, stages, 4), (2, stages, 4), (2, 4), (groups - 1,),
         (groups - 1,), (3, 6), (3, 6), (5,),
     ]
     return shapes, sems
@@ -796,7 +818,8 @@
     if local == 1 and groups == 4 * CORES and ndp == 4:
         slots = slot_capacity(count, expert_ids.shape[1], groups)
         shapes, _ = kernel_scratch(groups, ndp, pad16(slots), count, width, part, ff)
-        tiled = count % 32 == 0 and part % 128 == 0 and ff % 128 == 0 and 4 * slots > count
+        tiled = count % 32 == 0 and part % 128 == 0 and ff % 128 == 0
+        tiled = tiled and 4 * slots > count and pad16(CORES * slots) < count
         if tiled and scratch_bytes(shapes) < VMEM_MAX * 9 // 10:
             return line_body(groups, ndp, *args)
     return body(*args)

time: 115 us -> 114 us (level)
    pallas_call x1, Pallas kernels: 113 us -> 112 us  [line_body(): pl.pallas_call(functools.partial(moe_kernel, groups, ndp, cap, edge), out...]
where the time goes in v3:
time: 114 us
  Pallas kernels  113 us (99%)
    pallas_call x1, Pallas kernels, line_body(): pl.pallas_call(functools.partial(moe_kernel, groups, ndp, cap, edge), out...  112 us

profile of v3, /device:TPU:0, one launch (start us, length us, event | category | flops | bytes accessed | tf_op | source)
XLA Modules:
  0.0 113.8 jit_solution(412469607986567871)
XLA Ops:
  0.6 111.6 %shard_map.118 = (bf16[128,2048]{1,0:T(8,128)(2,1)S(1)}, bf16[128,2048]{1,0:T(8,128)(2,1)S(1)}, f32[2,128]{1,0:T(2,128)S(1)}, bf16[512,384]{1,0:T(8,128)(2,1)S(1...) custom-call(bf16[128,2048]{1,0:T(8,128)(2,1)} %tok_hbm.1, bf16[128,2048]{1,0:T(8,128)(2,1)} %grad_hbm.1, ...), custom_call_target="tpu_custom_call" | custom-call | tf_op jit(solution)/shard_map/pallas_call | solution.py:792
  112.2 1.4 %shard_map.119 = (bf16[128,2048]{1,0:T(8,128)(2,1)}, bf16[128,2048]{1,0:T(8,128)(2,1)}, f32[2,128]{1,0:T(2,128)}, bf16[512,384]{1,0:T(8,128)(2,1)}, bf16[512,384]{1,0:T(8,128)(2,1)}, /*index=5*/bf16[512,384]{1,0:T(8,128)(2,1)}) custom-call(bf16[128,2048]{1,0:T(8,128)(2,1)S(1)} %get-tuple-element.18.refs_0_, bf16[128,2048]{1,0:T(8,128)(2,1)S(1)} %get-tuple-element.19.refs_1_, ...), custom_call_target="tpu_custom_call" | custom-call | tf_op jit(solution)/shard_map/pallas_call | solution.py:715

commit v4 on v3

--- a/solution.py
+++ b/solution.py
@@ -176,26 +176,29 @@
         return jnp.where(first[i] > 0, ahead, number + lanes - ahead)
 
     hots = [one_hot(position(i), count) for i in range(2)]
-    dest = lax.broadcasted_iota(jnp.int32, (groups, count), 0) // CORES
-
-    def in_order(values, precision):
-        up, down = [
-            lax.dot_general(values, hot.astype(values.dtype), (((1,), (1,)), ((), ())),
-                            precision=precision, preferred_element_type=F32)
-            for hot in hots
-        ]
-        return jnp.where(dest >= chip, up, down)
-
-    slot_rows = in_order(slot.astype(BF16), None)
-    weight_rows = in_order(weight, lax.Precision.HIGHEST)
-    tiles = []
-    for e in range(groups):
-        other = e // CORES * CORES + (CORES - 1 - e % CORES)
-        row = lambda a, i: a[i:i + 1]
-        tiles.append(jnp.concatenate(
-            [row(slot_rows, e), row(weight_rows, e), row(slot_rows, other), row(slot, e), row(slot, other),
-             jnp.zeros((3, count), F32)], axis=0))
-    return tiles, hots[0].astype(BF16), hots[1].astype(BF16), hits
+    def tables():
+        dest = lax.broadcasted_iota(jnp.int32, (groups, count), 0) // CORES
+
+        def in_order(values, precision):
+            up, down = [
+                lax.dot_general(values, hot.astype(values.dtype), (((1,), (1,)), ((), ())),
+                                precision=precision, preferred_element_type=F32)
+                for hot in hots
+            ]
+            return jnp.where(dest >= chip, up, down)
+
+        slot_rows = in_order(slot.astype(BF16), None)
+        weight_rows = in_order(weight, lax.Precision.HIGHEST)
+        tiles = []
+        for e in range(groups):
+            other = e // CORES * CORES + (CORES - 1 - e % CORES)
+            row = lambda a, i: a[i:i + 1]
+            tiles.append(jnp.concatenate(
+                [row(slot_rows, e), row(weight_rows, e), row(slot_rows, other), row(slot, e), row(slot, other),
+                 jnp.zeros((3, count), F32)], axis=0))
+        return tiles
+
+    return tables, hots[0].astype(BF16), hots[1].astype(BF16), hits
 
 
 def one_hot(row, height):
@@ -313,9 +316,7 @@
         pl.semaphore_signal(barrier, inc=1, device_id={"dp": (dp + off) % ndp},
                             device_id_type=pl.DeviceIdType.MESH)
 
-    tiles, up_hot, down_hot, hits = route_tables(ids_ref[...], weight_ref[...], groups, chip)
-    for e in range(groups):
-        meta_own[e] = tiles[e]
+    tables, up_hot, down_hot, hits = route_tables(ids_ref[...], weight_ref[...], groups, chip)
 
     def arrange(t):
         value = (tok, grad)[t][...]
@@ -361,13 +362,15 @@
     depart_up(0, has_up)
     depart_down(0, has_down)
     depart_mate(0)
+    for i in range(2):
+        loads[1 + i].wait()
+        weight_direct(i)
+    for e, tile in enumerate(tables()):
+        meta_own[e] = tile
     for off in range(1, groups):
         other = (me + off) % groups
         send(None, meta_own.at[other], metas.at[me], meta_send.at[off - 1], meta_recv.at[off - 1],
              {"expert": other})
-    for i in range(2):
-        loads[1 + i].wait()
-        weight_direct(i)
     metas[me] = meta_own[me]
     if edge < count:
         rest = pl.ds(edge, count - edge)
@@ -588,8 +591,8 @@
             arrive(1, q, c, at_edge)
         compact(1, q)
     backward_hidden(range(last))
+    backward_rows(range(last))
     arrive(1, last, 1, inside)
-    backward_rows(range(last))
     give_back(0, last, False)
     for c in range(2):
         arrive(1, last, c, at_edge)
@@ -688,11 +691,16 @@
         for h in range(2):
             landed(grx.at[i, 2 + h], gr_recv.at[i, 2 + h])
             own[i, h] = own[i, h] + grx[i, 2 + h].astype(F32)
+
+    def finish_weights():
+        for i, ref in enumerate((gg_ref, ug_ref, dg_ref)):
+            for h in range(2):
+                landed(grx.at[i, 4 + h], gr_recv.at[i, 4 + h])
+                ref[halves[h]] = (own[i, h] + grx[i, 4 + h].astype(F32)).astype(BF16)
+
+    pl.when(inside)(finish_weights)
     finish(1, tgrad_ref)
-    for i, ref in enumerate((gg_ref, ug_ref, dg_ref)):
-        for h in range(2):
-            landed(grx.at[i, 4 + h], gr_recv.at[i, 4 + h])
-            ref[halves[h]] = (own[i, h] + grx[i, 4 + h].astype(F32)).astype(BF16)
+    pl.when(at_edge)(finish_weights)
     for cond, args in pending:
         if cond is None:
             copy(*args).wait_send()

time: 114 us -> 114 us (level)
  no operation moved by 1% of the time
where the time goes in v4:
time: 114 us
  Pallas kernels  113 us (99%)
    pallas_call x1, Pallas kernels, line_body(): pl.pallas_call(functools.partial(moe_kernel, groups, ndp, cap, edge), out...  112 us

profile of v4, /device:TPU:0, one launch (start us, length us, event | category | flops | bytes accessed | tf_op | source)
XLA Modules:
  0.0 113.8 jit_solution(809741242512174918)
XLA Ops:
  0.6 111.6 %shard_map.118 = (bf16[128,2048]{1,0:T(8,128)(2,1)S(1)}, bf16[128,2048]{1,0:T(8,128)(2,1)S(1)}, f32[2,128]{1,0:T(2,128)S(1)}, bf16[512,384]{1,0:T(8,128)(2,1)S(1...) custom-call(bf16[128,2048]{1,0:T(8,128)(2,1)} %tok_hbm.1, bf16[128,2048]{1,0:T(8,128)(2,1)} %grad_hbm.1, ...), custom_call_target="tpu_custom_call" | custom-call | tf_op jit(solution)/shard_map/pallas_call | solution.py:800
  112.2 1.4 %shard_map.119 = (bf16[128,2048]{1,0:T(8,128)(2,1)}, bf16[128,2048]{1,0:T(8,128)(2,1)}, f32[2,128]{1,0:T(2,128)}, bf16[512,384]{1,0:T(8,128)(2,1)}, bf16[512,384]{1,0:T(8,128)(2,1)}, /*index=5*/bf16[512,384]{1,0:T(8,128)(2,1)}) custom-call(bf16[128,2048]{1,0:T(8,128)(2,1)S(1)} %get-tuple-element.18.refs_0_, bf16[128,2048]{1,0:T(8,128)(2,1)S(1)} %get-tuple-element.19.refs_1_, ...), custom_call_target="tpu_custom_call" | custom-call | tf_op jit(solution)/shard_map/pallas_call | solution.py:723
